TPU v7x, 128 devices: a whole 4x4x4 slice. The times are simulated.
128 devices in a mesh: dp: 4 (over z), vocab: 32 (over y, x, core).
Axes of the slice: x: 4, y: 4, z: 4, core: 2. Of those that a mesh axis runs over, the one named last changes fastest.
Arguments:
- hidden: bfloat16 [2048, 5120], P('dp', 'vocab')
- weight: bfloat16 [5120, 77824], P(None, 'vocab'), may hold values from -0.078125 to 0.078125
- targets: int32 [2048], P('dp'), may hold values from 0 to 77823
- old_logprob: float32 [2048], P('dp'), may hold values from -13 to -10.5
- ref_logprob: float32 [2048], P('dp'), may hold values from -13 to -10.5
- lengths: int32 [32], P('dp'), may hold values from 1 to 64
- rewards: int32 [32], P('dp'), may hold values from 0 to 4
- group_ids: int32 [32], P('dp'), may hold values from 0 to 3, as said below
Outputs:
- token_logprob: float32 [2048], P('dp')
- entropy: float32 [2048], P('dp')
- advantage: float32 [2048], P('dp')
- loss: float32 [], replicated
Inputs may be any that keep to these rules, and one draw needn't show every extreme that they name: `group_ids`: each prompt number is named by exactly 8 rollouts.
All inputs are finite; a program needn't handle non-finite values.
Results may differ from a plain program's by a relative error of at most 0.0003.
Values may be sent and summed in bfloat16 or wider, within the bound.
No kernel may reach another device: no remote copies, remote signals or barrier semaphores. Data moves between devices by JAX's collectives and lax.ppermute only.
A program may use at most 128 MiB of HBM per device.

v0:
```python
import jax
import jax.numpy as jnp
from jax import lax
from jax.sharding import PartitionSpec as P

GROUP = 8


def from_everyone(value, axis):
    size = lax.axis_size(axis)
    return lax.all_to_all(
        jnp.broadcast_to(value[None], (size, *value.shape)), axis, 0, 0, tiled=True
    )


def collected_together(value, axis):
    leaves = jax.tree.leaves(value)
    turns = sorted(range(len(leaves)), key=lambda k: -leaves[k].size)
    width = (1, *leaves[turns[0]].shape)[-1]
    lines = [
        jnp.pad(leaves[k].reshape(-1), (0, -leaves[k].size % width)).reshape(-1, width)
        for k in turns
    ]
    both, at, found = (from_everyone(jnp.concatenate(lines), axis), 0, {})
    for k, line in zip(turns, lines):
        share = both[:, at : at + len(line)].reshape(len(both), -1)
        found[k] = share[:, : leaves[k].size].reshape(-1, *leaves[k].shape)
        at += len(line)
    numbers = iter(range(len(leaves)))
    return jax.tree.map(lambda _: found[next(numbers)], value)


def folded_in_pairs(pieces, combine):
    while len(jax.tree.leaves(pieces)[0]) > 1:
        pieces = jax.vmap(combine)(
            *(jax.tree.map(lambda part: part[side::2], pieces) for side in (0, 1))
        )
    return jax.tree.map(lambda part: part[0], pieces)


def merged(value, axis, combine):
    pieces = collected_together(value, axis)
    return folded_in_pairs(pieces, combine)


def over_copies(value, axis):
    everything = from_everyone(value, axis)
    return jnp.sum(everything, axis=0)


def together(arrays, axis):
    ends = [0]
    for a in arrays:
        ends.append(ends[-1] + a.size)
    total = over_copies(jnp.concatenate([a.ravel() for a in arrays]), axis)
    return tuple((total[b:e].reshape(a.shape) for a, b, e in zip(arrays, ends, ends[1:])))


def combine(first, second):
    top = jnp.maximum(first[0], second[0])
    scale_a = jnp.exp(first[0] - top)
    scale_b = jnp.exp(second[0] - top)
    return (
        top,
        first[1] * scale_a + second[1] * scale_b,
        first[2] * scale_a + second[2] * scale_b,
        first[3] + second[3],
    )


def per_device(hidden, weight, targets, old_logprob, ref_logprob, lengths, rewards, group_ids):
    width = weight.shape[1]
    tok_rows = hidden.shape[0]
    offset = lax.axis_index("vocab") * width
    features_all = lax.all_gather(hidden, "vocab", axis=1, tiled=True)
    logits = jnp.dot(features_all, weight, preferred_element_type=jnp.float32)
    columns = lax.broadcasted_iota(jnp.int32, (1, width), 1) + offset
    picked = jnp.sum(jnp.where(columns == targets[:, None], logits, 0.0), axis=1)
    local_top = jnp.max(logits, axis=1)
    scaled = jnp.exp(logits - local_top[:, None])
    top, total, moment, target_logit = merged(
        (local_top, jnp.sum(scaled, axis=1), jnp.sum(scaled * logits, axis=1), picked),
        "vocab",
        combine,
    )
    lse = top + jnp.log(total)
    token_logprob = target_logit - lse
    entropy = lse - moment / total
    roll_rows = rewards.shape[0]
    prompt_count = roll_rows * lax.axis_size("dp") // GROUP
    member = (group_ids[:, None] == jnp.arange(prompt_count, dtype=jnp.int32)[None, :]).astype(
        jnp.float32
    )
    scores = rewards.astype(jnp.float32)
    part_sums = jnp.dot(scores, member, precision=lax.Precision.HIGHEST)
    part_squares = jnp.dot(scores * scores, member, precision=lax.Precision.HIGHEST)
    seq_len = tok_rows // roll_rows
    position = jnp.arange(seq_len, dtype=jnp.int32)
    mask = (position[None, :] < lengths[:, None]).astype(jnp.float32).reshape(tok_rows)
    local_count = jnp.sum(mask)
    sums, squares = together((part_sums, part_squares), "dp")
    mean = sums / GROUP
    spread = jnp.sqrt(jnp.maximum(squares / GROUP - mean * mean, 0.0))
    mean_roll = jnp.dot(member, mean, precision=lax.Precision.HIGHEST)
    spread_roll = jnp.dot(member, spread, precision=lax.Precision.HIGHEST)
    advantage = jnp.repeat((scores - mean_roll) / jnp.maximum(spread_roll, 1.0), seq_len)
    ratio = jnp.exp(jnp.clip(token_logprob - old_logprob, -20.0, 20.0))
    surrogate = -jnp.minimum(ratio * advantage, jnp.clip(ratio, 0.8, 1.2) * advantage)
    shift = jnp.clip(ref_logprob - token_logprob, -20.0, 20.0)
    divergence = jnp.exp(shift) - shift - 1.0
    local_numer = jnp.sum(mask * (surrogate + 0.04 * divergence - 0.01 * entropy))
    numer, count = together((local_numer, local_count), "dp")
    loss = numer / count
    return (token_logprob, entropy, advantage, loss)


def solution(mesh):
    return jax.shard_map(
        per_device,
        mesh=mesh,
        in_specs=(
            P("dp", "vocab"),
            P(None, "vocab"),
            P("dp"),
            P("dp"),
            P("dp"),
            P("dp"),
            P("dp"),
            P("dp"),
        ),
        out_specs=(P("dp"), P("dp"), P("dp"), P()),
        check_vma=False,
    )
```

profile of v0, /device:TPU:0, one launch (start us, length us, event | category | flops | bytes accessed | tf_op | source)
XLA Modules:
  0.0 118.6 jit_solution(14122698012922345631)
XLA Ops:
  7.2 0.0 all-gather.2.cloned.1.call-start
  7.2 0.7 all-gather.2.cloned.1.call-update
  7.9 0.9 convolution_bitcast_fusion.2
  8.8 0.9 convolution_bitcast_fusion.3
  9.6 0.1 pad_maximum_fusion.1
  9.7 0.6 broadcast_in_dim.14
  10.3 5.4 %all-to-all-start.1 = ((f32[4,1,8]{2,1,0:T(1,128)}), f32[4,1,8]{2,1,0:T(1,128)S(1)}, u32[]{:S(2)}, u32[]{:S(2)}) async-start(f32[4,1,8]{2,1,0:T(1,128)} %broadcast_in_dim.14), calls=%async_computation.1 | async-start | bytes 4096 | tf_op jit(solution)/shard_map/all_to_all | solution.py:11
  15.7 1.3 %convert_reduce_fusion = f32[]{:T(128)} fusion(s32[8]{0:T(128)} %param.13), kind=kLoop, calls=%fused_computation.29 | loop fusion | flops 1535 | bytes 36 | tf_op jit(solution)/shard_map/reduce_sum | solution.py:100
  17.0 0.7 iota_compare_fusion
  17.8 0.1 lt.21
  17.9 3.1 %all-to-all-done.1 = f32[4,1,8]{2,1,0:T(1,128)S(1)} async-done(((f32[4,1,8]{2,1,0:T(1,128)}), f32[4,1,8]{2,1,0:T(1,128)S(1)}, u32[]{:S(2)}, u32[]{:S(2)}) %all-to-all-start.1) | async-done | bytes 160 | tf_op jit(solution)/shard_map/all_to_all | solution.py:11
  20.9 0.0 copy-start.3
  20.9 39.0 %all-gather.2.cloned.1.call-done = bf16[512,5120]{0,1:T(8,128)(2,1)} async-done(((bf16[512,160]{0,1:T(8,128)(2,1)}), bf16[512,5120]{0,1:T(8,128)(2,1)}) %all-gather.2.cloned.1.call-update) | async-done | bytes 5242896 | tf_op jit(solution)/shard_map/all_gather | solution.py:75
  59.9 19.3 %fusion.34 = (f32[512]{0:T(512)S(1)}, f32[512,2432]{1,0:T(8,128)S(1)}) fusion(bf16[512,5120]{0,1:T(8,128)(2,1)} %all-gather.2.cloned.1.call-done, bf16[5120,2432]{1,0:T(8,128)(2,1)} %param.9), kind=kOutput, calls=%fused_computation.81 | convolution fusion | flops 12751929344 | bytes 35129344 | tf_op jit(solution)/shard_map/dot_general | solution.py:76
  79.2 0.0 copy-start.6
  79.2 0.0 copy-start.7
  79.2 0.0 copy-start.4
  79.2 0.0 copy-start.5
  79.2 0.0 copy-done.3
  79.2 2.1 %fusion = (f32[512]{0:T(512)S(1)}, f32[512]{0:T(512)S(1)}, f32[512]{0:T(512)S(1)}) fusion(f32[512,2432]{1,0:T(8,128)S(1)} %get-tuple-element.24, f32[512]{0:T(512)S(1)} %get-tuple-element.23, s32[512]{0:T(512)S(1)} %copy-done.3, s32[2432]{0:T(1024)S(1)} %iota_add_fusion), kind=kLoop, calls=%fused_computation.3 | loop fusion | flops 8714752 | bytes 5000704 | tf_op jit(solution)/shard_map/reduce_sum | solution.py:82
  81.3 0.7 broadcast_in_dim.13
  82.0 5.0 %all-to-all-start = ((f32[32,4,512]{2,1,0:T(4,128)}), f32[32,4,512]{2,1,0:T(4,128)S(1)}, u32[]{:S(2)}, u32[]{:S(2)}) async-start(f32[32,4,512]{2,1,0:T(4,128)} %broadcast_in_dim.13), calls=%async_computation | async-start | bytes 524288 | tf_op jit(solution)/shard_map/all_to_all | solution.py:11
  87.1 0.0 copy-done.6
  87.1 0.2 fusion.3
  87.3 0.0 copy-done.7
  87.3 0.2 fusion.2
  87.5 0.1 broadcast_in_dim.15
  87.6 0.1 reshape.83
  87.6 0.0 copy-start
  87.6 8.2 %all-to-all-done = f32[32,4,512]{2,1,0:T(4,128)S(1)} async-done(((f32[32,4,512]{2,1,0:T(4,128)}), f32[32,4,512]{2,1,0:T(4,128)S(1)}, u32[]{:S(2)}, u32[]{:S(2)}) %all-to-all-start) | async-done | bytes 262176 | tf_op jit(solution)/shard_map/all_to_all | solution.py:11
  95.9 0.2 fusion.32
  97.0 0.0 copy-start.2
  97.1 0.0 copy-start.1
  97.1 0.0 copy-done.4
  97.1 0.0 copy-done.5
  97.1 0.7 fusion.18
  97.8 1.3 %pad_maximum_fusion.2 = f32[2]{0:T(128)S(1)} fusion(f32[1]{0:T(128)} %bitcast.19, f32[1]{0:T(128)} %bitcast.18), kind=kLoop, calls=%fused_computation.62 | loop fusion | flops 2 | bytes 16 | tf_op jit(solution)/shard_map/concatenate | solution.py:55
  99.2 9.5 %all_to_all.17 = f32[4,1,2]{2,1,0:T(1,128)S(1)} all-to-all(f32[4,1,2]{2,1,0:T(1,128)S(1)} %broadcast_in_dim.16), channel_id=1, replica_groups=mesh['dp'=4,'vocab'=32] {'dp'}, dimensions={0} | all-to-all | bytes 64 | tf_op jit(solution)/shard_map/all_to_all | solution.py:11
  108.7 0.6 fusion.33
  110.6 0.0 copy-done
  110.6 0.0 copy-done.2
  110.6 0.0 copy-done.1
  (53 shorter events, 1.0 us)
Async XLA Ops:
  7.2 52.7 %all-gather.2.cloned.1.call-start = ((), (), s32[]{:S(2)}) async-start(), calls=%async_computation.3 | async-start | bytes 5406720 | tf_op jit(solution)/shard_map/all_gather | solution.py:75
  10.3 10.6 %all-to-all-start.1 = ((f32[4,1,8]{2,1,0:T(1,128)}), f32[4,1,8]{2,1,0:T(1,128)S(1)}, u32[]{:S(2)}, u32[]{:S(2)}) async-start(f32[4,1,8]{2,1,0:T(1,128)} %broadcast_in_dim.14), calls=%async_computation.1 | async-start | bytes 4096 | tf_op jit(solution)/shard_map/all_to_all | solution.py:11
  20.9 58.3 %copy-start.3 = (s32[512]{0:T(512)S(1)}, s32[512]{0:T(512)}, u32[]{:S(2)}) copy-start(s32[512]{0:T(512)} %param.10) | copy-start | bytes 6148
  79.2 7.9 %copy-start.6 = (s32[8]{0:T(128)S(1)}, s32[8]{0:T(128)}, u32[]{:S(2)}) copy-start(s32[8]{0:T(128)} %param.15) | copy-start | bytes 100
  79.2 8.1 %copy-start.7 = (s32[8]{0:T(128)S(1)}, s32[8]{0:T(128)}, u32[]{:S(2)}) copy-start(s32[8]{0:T(128)} %param.14) | copy-start | bytes 100
  79.2 17.9 %copy-start.4 = (f32[512]{0:T(512)S(1)}, f32[512]{0:T(512)}, u32[]{:S(2)}) copy-start(f32[512]{0:T(512)} %param.12) | copy-start | bytes 6148
  79.2 17.9 %copy-start.5 = (f32[512]{0:T(512)S(1)}, f32[512]{0:T(512)}, u32[]{:S(2)}) copy-start(f32[512]{0:T(512)} %param.11) | copy-start | bytes 6148
  82.0 13.8 %all-to-all-start = ((f32[32,4,512]{2,1,0:T(4,128)}), f32[32,4,512]{2,1,0:T(4,128)S(1)}, u32[]{:S(2)}, u32[]{:S(2)}) async-start(f32[32,4,512]{2,1,0:T(4,128)} %broadcast_in_dim.13), calls=%async_computation | async-start | bytes 524288 | tf_op jit(solution)/shard_map/all_to_all | solution.py:11
  87.6 22.9 %copy-start = (f32[512]{0:T(512)}, f32[512]{0:T(512)S(1)}, u32[]{:S(2)}) copy-start(f32[512]{0:T(512)S(1)} %reshape.83) | copy-start | bytes 6148
  97.0 13.6 %copy-start.2 = (f32[1,512]{1,0:T(1,128)}, f32[1,512]{1,0:T(1,128)S(1)}, u32[]{:S(2)}) copy-start(f32[1,512]{1,0:T(1,128)S(1)} %get-tuple-element.7) | copy-start | bytes 6148
  97.1 13.5 %copy-start.1 = (f32[1,512]{1,0:T(1,128)}, f32[1,512]{1,0:T(1,128)S(1)}, u32[]{:S(2)}) copy-start(f32[1,512]{1,0:T(1,128)S(1)} %fusion.12) | copy-start | bytes 6148
Sparse Core Ops, SparseCore 0:
  10.2 49.6 all-gather.1
where the time goes:
time: 119 us
  waiting for transfers between devices  50.9 us (43%)
  matrix products  21.4 us (18%)
  between operations  16.7 us (14%)
  starting transfers between devices  10.5 us (9%)
  blocking collectives  9.49 us (8%)
  other arithmetic  6.53 us (5%)
  local copies, waits for them, and re-layouts  3.05 us (3%)
    all_gather x1, waiting for transfers between devices, per_device(): features_all = lax.all_gather(hidden, 'vocab', axis=1, tiled=True)  39 us
    dot_general x1, matrix products, per_device(): logits = jnp.dot(features_all, weight, preferred_element_type=jnp.float32)  19.3 us
    all_to_all x2, waiting for transfers between devices, from_everyone(): lax.all_to_all(jnp.broadcast_to(value[None], (size, *value.shape)), axis,...  11.3 us
    all_to_all x2, starting transfers between devices, from_everyone(): lax.all_to_all(jnp.broadcast_to(value[None], (size, *value.shape)), axis,...  10.4 us
    all_to_all x1, blocking collectives, from_everyone(): lax.all_to_all(jnp.broadcast_to(value[None], (size, *value.shape)), axis,...  9.49 us
  transfers between devices with their start and end apart: 3, of which 3 were waited for; matrix products, arithmetic and copies ran while one was open for 4% of the time, Pallas kernels for 0%

commit v1 on v0

v1 whole, which is shorter than its diff:
```python
import functools

import jax
import jax.numpy as jnp
from jax import lax
from jax.experimental import pallas as pl
from jax.experimental.pallas import tpu as pltpu
from jax.sharding import PartitionSpec as P

GROUP = 8
LANES = 128
SIDE = 4
STEPS = (0, -1, 1, 2)
F32 = jnp.float32


def device(y, x, core):
    return ((y % SIDE) * SIDE + x % SIDE) * 2 + core


def everyone():
    return [(v // (2 * SIDE), v // 2 % SIDE, v % 2) for v in range(2 * SIDE * SIDE)]


def send_on(value, phase, step):
    pairs = []
    for y, x, core in everyone():
        to = (y, x + step, core) if core == phase else (y + step, x, core)
        pairs.append((device(y, x, core), device(*to)))
    return lax.ppermute(value, "vocab", pairs)


def swap(value):
    pairs = [(device(y, x, core), device(y, x, 1 - core)) for y, x, core in everyone()]
    return lax.ppermute(value, "vocab", pairs)


def over_dp(value, mask):
    return lax.ppermute(value, "dp", [(v, v ^ mask) for v in range(lax.axis_size("dp"))])


def block_rows(second, partner, depth):
    v = lax.axis_index("vocab")
    core = (v & 1) ^ partner
    x, y = (v >> 1) & (SIDE - 1), v >> 3
    rows = []
    for first in STEPS:
        dx = jnp.where(core == 0, first, second)
        dy = jnp.where(core == 0, second, first)
        block = (((y + dy) & (SIDE - 1)) * SIDE + ((x + dx) & (SIDE - 1))) * 2 + core
        rows.append(pl.multiple_of(block * depth, 32))
    return rows


def column_tiles(width):
    return [(b, min(b + 512, width)) for b in range(0, width, 512)]


def load_kernel(lo, hi, *refs):
    w_ref, out, sems = refs[0], refs[-2], refs[-1]
    count = sems.shape[0]
    size = (hi - lo) // count
    copies = [
        pltpu.make_async_copy(
            w_ref.at[pl.ds(lo + k * size, size)], out.at[pl.ds(lo + k * size, size)], sems.at[k]
        )
        for k in range(count)
    ]
    for c in copies:
        c.start()
    for c in copies:
        c.wait()


def multiply(parts, depth, refs, acc_in, acc, lhs):
    w_ref = refs[-1]
    rows, at = [], 0
    for ref, part in zip(refs, parts):
        size = ref.shape[0]
        lhs[:, at : at + size] = ref[...].T
        rows += block_rows(*part, depth)
        at += size
    for b, e in column_tiles(w_ref.shape[1]):
        w = jnp.concatenate([w_ref[pl.ds(r, depth), b:e] for r in rows], axis=0)
        out = jnp.dot(lhs[...], w, preferred_element_type=F32)
        acc[:, b:e] = out if acc_in is None else acc_in[:, b:e] + out


def first_kernel(parts, depth, *refs):
    acc, _, lhs = refs[len(parts) + 1 :]
    multiply(parts, depth, refs[: len(parts) + 1], None, acc, lhs)


def middle_kernel(parts, depth, *refs):
    acc_in, acc, _, lhs = refs[len(parts) + 1 :]
    multiply(parts, depth, refs[: len(parts) + 1], acc_in, acc, lhs)


def last_kernel(parts, depth, *refs):
    acc_in, target, stats, acc, lhs = refs[len(parts) + 1 :]
    multiply(parts, depth, refs[: len(parts) + 1], acc_in, acc, lhs)
    tok, width = acc.shape
    step = 64
    tops, totals, moments, picks = [], [], [], []
    lane = lax.broadcasted_iota(jnp.int32, (step, LANES), 1) + lax.axis_index("vocab") * width
    for r in range(0, tok, step):
        want = target[r : r + step, :] - lane
        top = acc[r : r + step, 0:LANES]
        pick = jnp.where(want == 0, top, 0.0)
        for b in range(LANES, width, LANES):
            piece = acc[r : r + step, b : b + LANES]
            top = jnp.maximum(top, piece)
            pick = jnp.where(want == b, piece, pick)
        total = jnp.zeros_like(top)
        moment = jnp.zeros_like(top)
        for b in range(0, width, LANES):
            piece = acc[r : r + step, b : b + LANES]
            scaled = jnp.exp(piece - top)
            total += scaled
            moment += scaled * piece
        tops.append(top)
        totals.append(total)
        moments.append(moment)
        picks.append(pick)
    top, total, moment, pick = (
        jnp.concatenate(p, axis=0).T for p in (tops, totals, moments, picks)
    )
    best = jnp.max(top, axis=0, keepdims=True)
    scale = jnp.exp(top - best)
    stats[0:1, :] = best
    stats[1:2, :] = jnp.sum(total * scale, axis=0, keepdims=True)
    stats[2:3, :] = jnp.sum(moment * scale, axis=0, keepdims=True)
    stats[3:4, :] = jnp.sum(pick, axis=0, keepdims=True)


def in_vmem(value):
    return pltpu.with_memory_space_constraint(value, pltpu.VMEM)


def vmem_specs(count):
    return [pl.BlockSpec(memory_space=pltpu.VMEM)] * count


def load(weight, held, lo, hi, pieces):
    weight_there = pltpu.with_memory_space_constraint(weight, pltpu.HBM)
    operands = (weight_there,) if held is None else (weight_there, in_vmem(held))
    return pl.pallas_call(
        functools.partial(load_kernel, lo, hi),
        out_shape=pltpu.VMEM(weight.shape, weight.dtype),
        in_specs=[pl.BlockSpec(memory_space=pltpu.HBM), *vmem_specs(len(operands) - 1)],
        out_specs=pl.BlockSpec(memory_space=pltpu.VMEM),
        scratch_shapes=[pltpu.SemaphoreType.DMA((pieces,))],
        input_output_aliases={} if held is None else {1: 0},
        cost_estimate=pl.CostEstimate(flops=1 << 31, bytes_accessed=1 << 20, transcendentals=0),
        compiler_params=pltpu.CompilerParams(vmem_limit_bytes=16 << 20),
    )(*operands)


def matmul(kernel, blocks, parts, rest, weight, out_shape, extra=()):
    depth_sum = sum(b.shape[0] for b in blocks)
    rows, width = blocks[0].shape[1], weight.shape[1]
    depth = weight.shape[0] // lax.axis_size("vocab")
    operands = (*blocks, weight, *rest)
    aliases = {}
    if kernel is not last_kernel:
        out_shape = (out_shape, jax.ShapeDtypeStruct(weight.shape, weight.dtype))
        aliases = {len(blocks): 1} | ({len(blocks) + 1: 0} if rest else {})
    return pl.pallas_call(
        functools.partial(kernel, parts, depth),
        out_shape=out_shape,
        in_specs=vmem_specs(len(operands)),
        out_specs=jax.tree.map(lambda _: pl.BlockSpec(memory_space=pltpu.VMEM), out_shape),
        scratch_shapes=[*extra, pltpu.VMEM((rows, depth_sum), jnp.bfloat16)],
        input_output_aliases=aliases,
        cost_estimate=pl.CostEstimate(
            flops=2 * rows * depth_sum * width, bytes_accessed=1 << 20, transcendentals=0
        ),
        compiler_params=pltpu.CompilerParams(vmem_limit_bytes=16 << 20),
    )(*[in_vmem(o) for o in operands])


def merged(stats, groups):
    size = len(groups[0])
    lines = lax.all_to_all(
        jnp.broadcast_to(stats[None], (size, *stats.shape)),
        "vocab", 0, 0, axis_index_groups=groups, tiled=True,
    )
    top = jnp.max(lines[:, 0], axis=0)
    scale = jnp.exp(lines[:, 0] - top[None])
    return jnp.stack(
        [
            top,
            jnp.sum(lines[:, 1] * scale, axis=0),
            jnp.sum(lines[:, 2] * scale, axis=0),
            jnp.sum(lines[:, 3], axis=0),
        ]
    )


def per_device(hidden, weight, targets, old_logprob, ref_logprob, lengths, rewards, group_ids):
    width = weight.shape[1]
    tok_rows = hidden.shape[0]
    acc_shape = jax.ShapeDtypeStruct((tok_rows, width), F32)
    features = hidden.T
    line = [features]
    for step in (1, -1, 2):
        line.append(send_on(features, 0, step))
    held = load(weight, None, 0, 3072, 4)
    held = load(weight, held, 3072, 5120, 4)
    line = jnp.concatenate(line, axis=0)
    far = []
    for step in (1, -1, 2):
        far.append(send_on(line, 1, step))
    line_p = swap(line)
    acc, held = matmul(first_kernel, (line, line_p), ((0, 0), (0, 1)), (), held, acc_shape)
    far_p = []
    for k in range(3):
        far_p.append(swap(far[k]))
    acc, held = matmul(middle_kernel, far[:2], ((-1, 0), (1, 0)), (acc,), held, acc_shape)
    acc, held = matmul(middle_kernel, far_p[:2], ((-1, 1), (1, 1)), (acc,), held, acc_shape)
    acc, held = matmul(middle_kernel, far[2:], ((2, 0),), (acc,), held, acc_shape)
    wanted_column = jnp.broadcast_to(targets[:, None], (tok_rows, LANES))
    stats = matmul(
        last_kernel, far_p[2:], ((2, 1),), (acc, wanted_column), held,
        jax.ShapeDtypeStruct((4, tok_rows), F32),
        extra=(pltpu.VMEM((tok_rows, width), F32),),
    )
    roll_rows = rewards.shape[0]
    prompt_count = roll_rows * lax.axis_size("dp") // GROUP
    member = (
        group_ids[:, None] == jnp.arange(prompt_count, dtype=jnp.int32)[None, :]
    ).astype(F32)
    scores = rewards.astype(F32)
    seq_len = tok_rows // roll_rows
    token = lax.broadcasted_iota(jnp.int32, (roll_rows, tok_rows), 1)
    own = token // seq_len == lax.broadcasted_iota(jnp.int32, (roll_rows, tok_rows), 0)
    live = own & (token % seq_len < lengths[:, None])
    mask = jnp.sum(live.astype(F32), axis=0)
    sums = jnp.concatenate(
        [
            jnp.sum(scores[:, None] * member, axis=0),
            jnp.sum((scores * scores)[:, None] * member, axis=0),
            jnp.sum(mask)[None],
            jnp.zeros((LANES - 2 * prompt_count - 1,), F32),
        ]
    )[None]
    sums = sums + over_dp(sums, 1)
    sums = sums + over_dp(sums, 3)

    rows = [[device(y, x, c) for x in range(SIDE) for c in range(2)] for y in range(SIDE)]
    columns = [[device(y, x, c) for y in range(SIDE)] for x in range(SIDE) for c in range(2)]
    stats = merged(merged(stats, rows), columns)
    top, total, moment, target_logit = stats
    lse = top + jnp.log(total)
    token_logprob = target_logit - lse
    entropy = lse - moment / total

    mean = sums[0, :prompt_count] / GROUP
    squares = sums[0, prompt_count : 2 * prompt_count]
    count = sums[0, 2 * prompt_count]
    spread = jnp.sqrt(jnp.maximum(squares / GROUP - mean * mean, 0.0))
    mean_roll = jnp.sum(member * mean[None, :], axis=1)
    spread_roll = jnp.sum(member * spread[None, :], axis=1)
    advantage = (scores - mean_roll) / jnp.maximum(spread_roll, 1.0)
    advantage = jnp.sum(jnp.where(own, advantage[:, None], 0.0), axis=0)
    ratio = jnp.exp(jnp.clip(token_logprob - old_logprob, -20.0, 20.0))
    surrogate = -jnp.minimum(ratio * advantage, jnp.clip(ratio, 0.8, 1.2) * advantage)
    shift = jnp.clip(ref_logprob - token_logprob, -20.0, 20.0)
    divergence = jnp.exp(shift) - shift - 1.0
    numer = jnp.sum(mask * (surrogate + 0.04 * divergence - 0.01 * entropy))
    numer = jnp.broadcast_to(numer, (1, LANES))
    numer = numer + over_dp(numer, 1)
    numer = numer + over_dp(numer, 3)
    loss = numer[0, 0] / count
    return (token_logprob, entropy, advantage, loss)


def solution(mesh):
    return jax.shard_map(
        per_device,
        mesh=mesh,
        in_specs=(
            P("dp", "vocab"),
            P(None, "vocab"),
            P("dp"),
            P("dp"),
            P("dp"),
            P("dp"),
            P("dp"),
            P("dp"),
        ),
        out_specs=(P("dp"), P("dp"), P("dp"), P()),
        check_vma=False,
    )
```

time: 119 us -> 85.3 us (0.72)
  waiting for transfers between devices: 50.9 us -> 16 us
  Pallas kernels: 0 us -> 27.4 us
  matrix products: 21.4 us -> 0 us
  starting transfers between devices: 10.5 us -> 27.2 us
  between operations: 16.7 us -> 2.8 us
  blocking collectives: 9.49 us -> 0 us
  other arithmetic: 6.53 us -> 8.8 us
    all_gather x1 -> x0, waiting for transfers between devices: 39 us -> none  [per_device(): features_all = lax.all_gather(hidden, 'vocab', axis=1, tiled=True)]
    pallas_call x0 -> x7, Pallas kernels: none -> 27.4 us  [the longest x5 18.1 us: matmul(): pl.pallas_call(functools.partial(kernel, parts, depth), out_shape=out_sha...]
    dot_general x5 -> x0, matrix products: 21.4 us -> none  [the longest x1 19.3 us: per_device(): logits = jnp.dot(features_all, weight, preferred_element_type=jnp.float32)]
    ppermute x0 -> x14, starting transfers between devices: none -> 20.6 us  [the longest x6 10.6 us: send_on(): return lax.ppermute(value, 'vocab', pairs)]
    all_to_all x1 -> x0, blocking collectives: 9.49 us -> none  [from_everyone(): lax.all_to_all(jnp.broadcast_to(value[None], (size, *value.shape)), axis,...]
    ppermute x0 -> x14, waiting for transfers between devices: none -> 5.14 us  [the longest x4 3.59 us: over_dp(): lax.ppermute(value, 'dp', [(v, v ^ mask) for v in range(lax.axis_size('dp...]
    all_to_all x2, starting transfers between devices: 10.4 us -> 6.61 us  [merged(): lax.all_to_all(jnp.broadcast_to(stats[None], (size, *stats.shape)), 'voca...]
    add x13 -> x5, other arithmetic: 0.18 us -> 2.03 us  [the longest x1 0.72 us: per_device(): sums = sums + over_dp(sums, 1)]
  transfers between devices with their start and end apart: 3 -> 16, of which waited for: 3 -> 5; matrix products, arithmetic and copies ran while one was open for 4% -> 8% of each run, Pallas kernels for 0% -> 27%
where the time goes in v1:
time: 85.3 us; the launch traced here: 84.9 us
  Pallas kernels  27.4 us (32%)
  starting transfers between devices  27.2 us (32%)
  waiting for transfers between devices  16 us (19%)
  other arithmetic  8.8 us (10%)
  between operations  2.8 us (3%)
  local copies, waits for them, and re-layouts  2.7 us (3%)
    pallas_call x5, Pallas kernels, matmul(): pl.pallas_call(functools.partial(kernel, parts, depth), out_shape=out_sha...  18.1 us
    all_to_all x2, waiting for transfers between devices, merged(): lax.all_to_all(jnp.broadcast_to(stats[None], (size, *stats.shape)), 'voca...  10.9 us
    ppermute x6, starting transfers between devices, send_on(): return lax.ppermute(value, 'vocab', pairs)  10.6 us
    ppermute x4, starting transfers between devices, over_dp(): lax.ppermute(value, 'dp', [(v, v ^ mask) for v in range(lax.axis_size('dp...  9.34 us
    pallas_call x2, Pallas kernels, load(): pl.pallas_call(functools.partial(load_kernel, lo, hi), out_shape=pltpu.VM...  9.3 us
    all_to_all x2, starting transfers between devices, merged(): lax.all_to_all(jnp.broadcast_to(stats[None], (size, *stats.shape)), 'voca...  6.61 us
    ppermute x4, waiting for transfers between devices, over_dp(): lax.ppermute(value, 'dp', [(v, v ^ mask) for v in range(lax.axis_size('dp...  3.59 us
  transfers between devices with their start and end apart: 16, of which 5 were waited for; matrix products, arithmetic and copies ran while one was open for 8% of the time, Pallas kernels for 27%

profile of v1, /device:TPU:0, one launch (start us, length us, event | category | flops | bytes accessed | tf_op | source)
XLA Modules:
  0.0 84.9 jit_solution(11734516317303058297)
XLA Ops:
  0.6 1.7 %collective-permute-start = (bf16[160,512]{1,0:T(8,128)(2,1)}, bf16[160,512]{1,0:T(8,128)(2,1)S(1)}, u32[]{:S(2)}, u32[]{:S(2)}) collective-permute-start(bf16[160,512]{1,0:T(8,128)(2,1)} %bitcast.56), channel_id=1, source_target_pairs={{0,2},{1,9},{2,4},{3,11},{4,6},{5,13},{6,0},{7,15},{8,10},{9,17},{... | collective-permute-start | bytes 491528 | tf_op jit(solution)/shard_map/ppermute | solution.py:30
  2.3 1.6 %collective-permute-start.1 = (bf16[160,512]{1,0:T(8,128)(2,1)}, bf16[160,512]{1,0:T(8,128)(2,1)S(1)}, u32[]{:S(2)}, u32[]{:S(2)}) collective-permute-start(bf16[160,512]{1,0:T(8,128)(2,1)} %bitcast.57), channel_id=1, source_target_pairs={{0,6},{1,25},{2,0},{3,27},{4,2},{5,29},{6,4},{7,31},{8,14},{9,1},{... | collective-permute-start | bytes 491528 | tf_op jit(solution)/shard_map/ppermute | solution.py:30
  3.9 1.9 %collective-permute-start.2 = (bf16[160,512]{1,0:T(8,128)(2,1)}, bf16[160,512]{1,0:T(8,128)(2,1)S(1)}, u32[]{:S(2)}, u32[]{:S(2)}) collective-permute-start(bf16[160,512]{1,0:T(8,128)(2,1)} %bitcast.58), channel_id=1, source_target_pairs={{0,4},{1,17},{2,6},{3,19},{4,0},{5,21},{6,2},{7,23},{8,12},{9,25},... | collective-permute-start | bytes 491528 | tf_op jit(solution)/shard_map/ppermute | solution.py:30
  5.9 0.7 convert_element_type.7
  6.5 0.7 convert_multiply_fusion
  7.2 1.3 %convert_reduce_fusion = (f32[512]{0:T(512)S(1)}, f32[]{:T(128)}) fusion(s32[8]{0:T(128)} %param.13, s32[512]{0:T(512)S(1)} %get-tuple-element.50, s32[512]{0:T(512)S(1)} %get-tuple-element.51, pred[512]{0:T(512)(128)(4,1)S(1)} %get-tuple-element.54, s32[512]{0:T(512)S(1)} %get-tuple-element.49, s32[512]{0:T(512)S(1)} %get-tuple-element.52, ...), kind=kLoop, calls=%fused_computation.1 | loop fusion | flops 32255 | bytes 11300 | tf_op jit(solution)/shard_map/reduce_sum | solution.py:238
  8.5 0.8 select_reduce_fusion.4
  9.3 0.7 maximum_bitcast_fusion
  10.1 1.9 %collective-permute-start.10 = (f32[1,128]{1,0:T(1,128)S(1)}, f32[1,128]{1,0:T(1,128)S(1)}, u32[]{:S(2)}, u32[]{:S(2)}) collective-permute-start(f32[1,128]{1,0:T(1,128)S(1)} %maximum_bitcast_fusion), channel_id=1, source_target_pairs={{0,32},{32,0},{64,96},{96,64},{1,33},{33,1},{65,97},{97,65},{2,34}... | collective-permute-start | bytes 1544 | tf_op jit(solution)/shard_map/ppermute | solution.py:39
  12.0 0.0 collective-permute-done
  12.0 0.0 collective-permute-done.1
  12.0 0.0 collective-permute-done.2
  12.0 1.0 %pad_maximum_fusion.refs_0_ = bf16[640,512]{1,0:T(8,128)(2,1)S(1)} fusion(bf16[160,512]{1,0:T(8,128)(2,1)S(1)} %collective-permute-done.2, bf16[160,512]{1,0:T(8,128)(2,1)S(1)} %collective-permute-done.1, bf16[160,512]{1,0:T(8,128)(2,1)S(1)} %collective-permute-done, bf16[160,512]{1,0:T(8,128)(2,1)} %bitcast.59), kind=kLoop, calls=%fused_computation | loop fusion | flops 2621440 | bytes 1310720 | tf_op jit(solution)/shard_map/concatenate | solution.py:210
  13.0 1.6 %collective-permute-start.5 = (bf16[640,512]{1,0:T(8,128)(2,1)S(1)}, bf16[640,512]{1,0:T(8,128)(2,1)S(1)}, u32[]{:S(2)}, u32[]{:S(2)}) collective-permute-start(bf16[640,512]{1,0:T(8,128)(2,1)S(1)} %pad_maximum_fusion.refs_0_), channel_id=1, source_target_pairs={{0,8},{1,3},{2,10},{3,5},{4,12},{5,7},{6,14},{7,1},{8,16},{9,11},{... | collective-permute-start | bytes 1966088 | tf_op jit(solution)/shard_map/ppermute | solution.py:30
  14.6 1.7 %collective-permute-start.7 = (bf16[640,512]{1,0:T(8,128)(2,1)S(1)}, bf16[640,512]{1,0:T(8,128)(2,1)S(1)}, u32[]{:S(2)}, u32[]{:S(2)}) collective-permute-start(bf16[640,512]{1,0:T(8,128)(2,1)S(1)} %pad_maximum_fusion.refs_0_), channel_id=1, source_target_pairs={{0,24},{1,7},{2,26},{3,1},{4,28},{5,3},{6,30},{7,5},{8,0},{9,15},{... | collective-permute-start | bytes 1966088 | tf_op jit(solution)/shard_map/ppermute | solution.py:30
  16.3 5.4 %shard_map.111.refs_1_ = bf16[5120,2432]{1,0:T(8,128)(2,1)S(1)} custom-call(bf16[5120,2432]{1,0:T(8,128)(2,1)} %refs_0_.3), custom_call_target="tpu_custom_call" | custom-call | flops 2147483648 | bytes 1048576 | tf_op jit(solution)/shard_map/pallas_call | solution.py:147
  21.6 0.1 collective-permute-start.9
  21.7 2.1 %collective-permute-start.3 = (bf16[640,512]{1,0:T(8,128)(2,1)S(1)}, bf16[640,512]{1,0:T(8,128)(2,1)S(1)}, u32[]{:S(2)}, u32[]{:S(2)}) collective-permute-start(bf16[640,512]{1,0:T(8,128)(2,1)S(1)} %pad_maximum_fusion.refs_0_), channel_id=1, source_target_pairs={{0,16},{1,5},{2,18},{3,7},{4,20},{5,1},{6,22},{7,3},{8,24},{9,13},... | collective-permute-start | bytes 1966088 | tf_op jit(solution)/shard_map/ppermute | solution.py:30
  23.8 0.0 collective-permute-done.10
  23.8 0.7 fusion.29
  24.5 3.1 %collective-permute-start.11 = (f32[1,128]{1,0:T(1,128)S(1)}, f32[1,128]{1,0:T(1,128)S(1)}, u32[]{:S(2)}, u32[]{:S(2)}) collective-permute-start(f32[1,128]{1,0:T(1,128)S(1)} %fusion.29), channel_id=1, source_target_pairs={{0,96},{32,64},{64,32},{96,0},{1,97},{33,65},{65,33},{97,1},{2,98}... | collective-permute-start | bytes 1544 | tf_op jit(solution)/shard_map/ppermute | solution.py:39
  27.7 3.9 %shard_map.112.refs_2_ = bf16[5120,2432]{1,0:T(8,128)(2,1)S(1)} custom-call(bf16[5120,2432]{1,0:T(8,128)(2,1)} %refs_0_.3, bf16[5120,2432]{1,0:T(8,128)(2,1)S(1)} %shard_map.111.refs_1_), custom_call_target="tpu_custom_call", output_to_operand_aliasing={{}: (1, {})} | custom-call | flops 2147483648 | bytes 1048576 | tf_op jit(solution)/shard_map/pallas_call | solution.py:147
  31.6 0.0 collective-permute-done.11
  31.6 0.1 sqrt_bitcast_fusion
  31.7 0.0 collective-permute-done.5.refs_0_
  31.7 0.1 collective-permute-start.6
  31.8 0.0 collective-permute-done.7.refs_1_
  31.8 0.5 collective-permute-start.8
  32.3 0.0 copy-done.2
  32.3 0.1 select_reduce_fusion.2
  32.4 1.5 %collective-permute-done.3.refs_0_ = bf16[640,512]{1,0:T(8,128)(2,1)S(1)} collective-permute-done((bf16[640,512]{1,0:T(8,128)(2,1)S(1)}, bf16[640,512]{1,0:T(8,128)(2,1)S(1)}, u32[]{:S(2)}, u32[]{:S(2)}) %collective-permute-start.3) | collective-permute-done | bytes 655392 | tf_op jit(solution)/shard_map/ppermute | solution.py:30
  33.9 0.0 collective-permute-start.4
  33.9 0.0 collective-permute-done.9.refs_1_
  33.9 3.6 %shard_map.113 = (f32[512,2432]{1,0:T(8,128)S(1)}, bf16[5120,2432]{1,0:T(8,128)(2,1)S(1)}) custom-call(bf16[640,512]{1,0:T(8,128)(2,1)S(1)} %pad_maximum_fusion.refs_0_, bf16[640,512]{1,0:T(8,128)(2,1)S(1)} %collective-permute-done.9.refs_1_, bf16[5120,2432]{1,0:T(8,128)(2,1)S(1)} %shard_map.112.refs_2_), custom_call_target="tpu_custom_call", output_to_operand_aliasing={{1}: (2, {})} | custom-call | flops 3187671040 | bytes 1048576 | tf_op jit(solution)/shard_map/pallas_call | solution.py:168
  37.5 3.7 %shard_map.114 = (f32[512,2432]{1,0:T(8,128)S(1)}, bf16[5120,2432]{1,0:T(8,128)(2,1)S(1)}) custom-call(bf16[640,512]{1,0:T(8,128)(2,1)S(1)} %collective-permute-done.5.refs_0_, bf16[640,512]{1,0:T(8,128)(2,1)S(1)} %collective-permute-done.7.refs_1_, bf16[5120,2432]{1,0:T(8,128)(2,1)S(1)} %get-tuple-element.12.refs_2_, ...), custom_call_target="tpu_custom_call", output_to_operand_aliasing={{1}: (2, {}), {0}: (3, {})} | custom-call | flops 3187671040 | bytes 1048576 | tf_op jit(solution)/shard_map/pallas_call | solution.py:168
  41.3 0.0 collective-permute-done.6.refs_0_
  41.3 0.0 collective-permute-done.8.refs_1_
  41.3 3.8 %shard_map.115 = (f32[512,2432]{1,0:T(8,128)S(1)}, bf16[5120,2432]{1,0:T(8,128)(2,1)S(1)}) custom-call(bf16[640,512]{1,0:T(8,128)(2,1)S(1)} %collective-permute-done.6.refs_0_, bf16[640,512]{1,0:T(8,128)(2,1)S(1)} %collective-permute-done.8.refs_1_, bf16[5120,2432]{1,0:T(8,128)(2,1)S(1)} %get-tuple-element.14.refs_2_, ...), custom_call_target="tpu_custom_call", output_to_operand_aliasing={{1}: (2, {}), {0}: (3, {})} | custom-call | flops 3187671040 | bytes 1048576 | tf_op jit(solution)/shard_map/pallas_call | solution.py:168
  45.1 0.0 copy-start.1
  45.1 2.7 %shard_map.116 = (f32[512,2432]{1,0:T(8,128)S(1)}, bf16[5120,2432]{1,0:T(8,128)(2,1)S(1)}) custom-call(bf16[640,512]{1,0:T(8,128)(2,1)S(1)} %collective-permute-done.3.refs_0_, bf16[5120,2432]{1,0:T(8,128)(2,1)S(1)} %get-tuple-element.16.refs_1_, f32[512,2432]{1,0:T(8,128)S(1)} %get-tuple-element.17.refs_2_), custom_call_target="tpu_custom_call", output_to_operand_aliasing={{1}: (1, {}), {0}: (2, {})} | custom-call | flops 1593835520 | bytes 1048576 | tf_op jit(solution)/shard_map/pallas_call | solution.py:168
  47.9 0.0 collective-permute-done.4.refs_0_
  47.9 0.1 broadcast_in_dim.22.refs_3_
  48.0 0.0 copy-start.5
  48.0 0.0 copy-start.3
  48.1 0.0 copy-start.4
  48.1 4.2 %shard_map.117 = f32[4,512]{1,0:T(4,128)S(1)} custom-call(bf16[640,512]{1,0:T(8,128)(2,1)S(1)} %collective-permute-done.4.refs_0_, bf16[5120,2432]{1,0:T(8,128)(2,1)S(1)} %get-tuple-element.18.refs_1_, f32[512,2432]{1,0:T(8,128)S(1)} %get-tuple-element.19.refs_2_, s32[512,128]{1,0:T(8,128)S(1)} %broadcast_in_dim.22.refs_3_), custom_call_target="tpu_custom_call" | custom-call | flops 1593835520 | bytes 1048576 | tf_op jit(solution)/shard_map/pallas_call | solution.py:168
  52.2 0.6 broadcast_in_dim.23
  52.9 3.3 %all-to-all-start = ((f32[8,4,512]{2,1,0:T(4,128)}), f32[8,4,512]{2,1,0:T(4,128)S(1)}, u32[]{:S(2)}, u32[]{:S(2)}) async-start(f32[8,4,512]{2,1,0:T(4,128)} %broadcast_in_dim.23), calls=%async_computation | async-start | bytes 131072 | tf_op jit(solution)/shard_map/all_to_all | solution.py:184
  56.3 5.5 %all-to-all-done = f32[8,4,512]{2,1,0:T(4,128)S(1)} async-done(((f32[8,4,512]{2,1,0:T(4,128)}), f32[8,4,512]{2,1,0:T(4,128)S(1)}, u32[]{:S(2)}, u32[]{:S(2)}) %all-to-all-start) | async-done | bytes 65568 | tf_op jit(solution)/shard_map/all_to_all | solution.py:184
  61.8 0.1 fusion.26
  61.9 0.6 broadcast_in_dim.24
  62.5 3.3 %all-to-all-start.1 = ((f32[4,4,512]{2,1,0:T(4,128)}), f32[4,4,512]{2,1,0:T(4,128)S(1)}, u32[]{:S(2)}, u32[]{:S(2)}) async-start(f32[4,4,512]{2,1,0:T(4,128)} %broadcast_in_dim.24), calls=%async_computation.1 | async-start | bytes 65536 | tf_op jit(solution)/shard_map/all_to_all | solution.py:184
  65.8 0.1 select_reduce_fusion
  65.9 5.3 %all-to-all-done.1 = f32[4,4,512]{2,1,0:T(4,128)S(1)} async-done(((f32[4,4,512]{2,1,0:T(4,128)}), f32[4,4,512]{2,1,0:T(4,128)S(1)}, u32[]{:S(2)}, u32[]{:S(2)}) %all-to-all-start.1) | async-done | bytes 32800 | tf_op jit(solution)/shard_map/all_to_all | solution.py:184
  71.3 0.0 copy-done.3
  71.3 1.2 %fusion.22 = (f32[]{:T(128)}, f32[512]{0:T(512)}, f32[512]{0:T(512)}) fusion(f32[512]{0:T(512)S(1)} %get-tuple-element.28, f32[512]{0:T(512)S(1)} %copy-done.3, f32[512]{0:T(512)S(1)} %select_reduce_fusion, f32[512]{0:T(512)S(1)} %copy-done.4, f32[512]{0:T(512)S(1)} %get-tuple-element.26, f32[512]{0:T(512)S(1)} %get-tuple-element.27, ...), kind=kLoop, calls=%fused_computation.48 | loop fusion | flops 10751 | bytes 20484 | tf_op jit(solution)/shard_map/reduce_sum | solution.py:270
  72.5 0.6 broadcast_in_dim.60
  73.1 1.1 %collective-permute-start.12 = (f32[1,128]{1,0:T(1,128)S(1)}, f32[1,128]{1,0:T(1,128)S(1)}, u32[]{:S(2)}, u32[]{:S(2)}) collective-permute-start(f32[1,128]{1,0:T(1,128)S(1)} %broadcast_in_dim.60), channel_id=1, source_target_pairs={{0,32},{32,0},{64,96},{96,64},{1,33},{33,1},{65,97},{97,65},{2,34}... | collective-permute-start | bytes 1544 | tf_op jit(solution)/shard_map/ppermute | solution.py:39
  74.2 2.6 %collective-permute-done.12 = f32[1,128]{1,0:T(1,128)S(1)} collective-permute-done((f32[1,128]{1,0:T(1,128)S(1)}, f32[1,128]{1,0:T(1,128)S(1)}, u32[]{:S(2)}, u32[]{:S(2)}) %collective-permute-start.12) | collective-permute-done | bytes 544 | tf_op jit(solution)/shard_map/ppermute | solution.py:39
  76.8 0.6 broadcast_add_fusion.1
  77.4 3.2 %collective-permute-start.13 = (f32[1,128]{1,0:T(1,128)S(1)}, f32[1,128]{1,0:T(1,128)S(1)}, u32[]{:S(2)}, u32[]{:S(2)}) collective-permute-start(f32[1,128]{1,0:T(1,128)S(1)} %broadcast_add_fusion.1), channel_id=1, source_target_pairs={{0,96},{32,64},{64,32},{96,0},{1,97},{33,65},{65,33},{97,1},{2,98}... | collective-permute-start | bytes 1544 | tf_op jit(solution)/shard_map/ppermute | solution.py:39
  80.6 0.7 slice.49
  81.3 1.0 %collective-permute-done.13 = f32[1,128]{1,0:T(1,128)S(1)} collective-permute-done((f32[1,128]{1,0:T(1,128)S(1)}, f32[1,128]{1,0:T(1,128)S(1)}, u32[]{:S(2)}, u32[]{:S(2)}) %collective-permute-start.13) | collective-permute-done | bytes 544 | tf_op jit(solution)/shard_map/ppermute | solution.py:39
  82.3 0.6 fusion.28
  (16 shorter events, 0.2 us)
Async XLA Ops:
  0.6 11.4 %collective-permute-start = (bf16[160,512]{1,0:T(8,128)(2,1)}, bf16[160,512]{1,0:T(8,128)(2,1)S(1)}, u32[]{:S(2)}, u32[]{:S(2)}) collective-permute-start(bf16[160,512]{1,0:T(8,128)(2,1)} %bitcast.56), channel_id=1, source_target_pairs={{0,2},{1,9},{2,4},{3,11},{4,6},{5,13},{6,0},{7,15},{8,10},{9,17},{... | collective-permute-start | bytes 491528 | tf_op jit(solution)/shard_map/ppermute | solution.py:30
  2.3 9.7 %collective-permute-start.1 = (bf16[160,512]{1,0:T(8,128)(2,1)}, bf16[160,512]{1,0:T(8,128)(2,1)S(1)}, u32[]{:S(2)}, u32[]{:S(2)}) collective-permute-start(bf16[160,512]{1,0:T(8,128)(2,1)} %bitcast.57), channel_id=1, source_target_pairs={{0,6},{1,25},{2,0},{3,27},{4,2},{5,29},{6,4},{7,31},{8,14},{9,1},{... | collective-permute-start | bytes 491528 | tf_op jit(solution)/shard_map/ppermute | solution.py:30
  3.9 8.1 %collective-permute-start.2 = (bf16[160,512]{1,0:T(8,128)(2,1)}, bf16[160,512]{1,0:T(8,128)(2,1)S(1)}, u32[]{:S(2)}, u32[]{:S(2)}) collective-permute-start(bf16[160,512]{1,0:T(8,128)(2,1)} %bitcast.58), channel_id=1, source_target_pairs={{0,4},{1,17},{2,6},{3,19},{4,0},{5,21},{6,2},{7,23},{8,12},{9,25},... | collective-permute-start | bytes 491528 | tf_op jit(solution)/shard_map/ppermute | solution.py:30
  10.1 13.7 %collective-permute-start.10 = (f32[1,128]{1,0:T(1,128)S(1)}, f32[1,128]{1,0:T(1,128)S(1)}, u32[]{:S(2)}, u32[]{:S(2)}) collective-permute-start(f32[1,128]{1,0:T(1,128)S(1)} %maximum_bitcast_fusion), channel_id=1, source_target_pairs={{0,32},{32,0},{64,96},{96,64},{1,33},{33,1},{65,97},{97,65},{2,34}... | collective-permute-start | bytes 1544 | tf_op jit(solution)/shard_map/ppermute | solution.py:39
  13.0 18.8 %collective-permute-start.5 = (bf16[640,512]{1,0:T(8,128)(2,1)S(1)}, bf16[640,512]{1,0:T(8,128)(2,1)S(1)}, u32[]{:S(2)}, u32[]{:S(2)}) collective-permute-start(bf16[640,512]{1,0:T(8,128)(2,1)S(1)} %pad_maximum_fusion.refs_0_), channel_id=1, source_target_pairs={{0,8},{1,3},{2,10},{3,5},{4,12},{5,7},{6,14},{7,1},{8,16},{9,11},{... | collective-permute-start | bytes 1966088 | tf_op jit(solution)/shard_map/ppermute | solution.py:30
  14.6 17.2 %collective-permute-start.7 = (bf16[640,512]{1,0:T(8,128)(2,1)S(1)}, bf16[640,512]{1,0:T(8,128)(2,1)S(1)}, u32[]{:S(2)}, u32[]{:S(2)}) collective-permute-start(bf16[640,512]{1,0:T(8,128)(2,1)S(1)} %pad_maximum_fusion.refs_0_), channel_id=1, source_target_pairs={{0,24},{1,7},{2,26},{3,1},{4,28},{5,3},{6,30},{7,5},{8,0},{9,15},{... | collective-permute-start | bytes 1966088 | tf_op jit(solution)/shard_map/ppermute | solution.py:30
  21.6 12.3 %collective-permute-start.9 = (bf16[640,512]{1,0:T(8,128)(2,1)S(1)}, bf16[640,512]{1,0:T(8,128)(2,1)S(1)}, u32[]{:S(2)}, u32[]{:S(2)}) collective-permute-start(bf16[640,512]{1,0:T(8,128)(2,1)S(1)} %pad_maximum_fusion.refs_0_), channel_id=1, source_target_pairs={{0,1},{1,0},{2,3},{3,2},{4,5},{5,4},{6,7},{7,6},{8,9},{9,8},{10,11... | collective-permute-start | bytes 1966088 | tf_op jit(solution)/shard_map/ppermute | solution.py:35
  21.7 12.2 %collective-permute-start.3 = (bf16[640,512]{1,0:T(8,128)(2,1)S(1)}, bf16[640,512]{1,0:T(8,128)(2,1)S(1)}, u32[]{:S(2)}, u32[]{:S(2)}) collective-permute-start(bf16[640,512]{1,0:T(8,128)(2,1)S(1)} %pad_maximum_fusion.refs_0_), channel_id=1, source_target_pairs={{0,16},{1,5},{2,18},{3,7},{4,20},{5,1},{6,22},{7,3},{8,24},{9,13},... | collective-permute-start | bytes 1966088 | tf_op jit(solution)/shard_map/ppermute | solution.py:30
  24.5 7.8 %copy-start.2 = (s32[8]{0:T(128)S(1)}, s32[8]{0:T(128)}, u32[]{:S(2)}) copy-start(s32[8]{0:T(128)} %param.15) | copy-start | bytes 100
  24.5 7.1 %collective-permute-start.11 = (f32[1,128]{1,0:T(1,128)S(1)}, f32[1,128]{1,0:T(1,128)S(1)}, u32[]{:S(2)}, u32[]{:S(2)}) collective-permute-start(f32[1,128]{1,0:T(1,128)S(1)} %fusion.29), channel_id=1, source_target_pairs={{0,96},{32,64},{64,32},{96,0},{1,97},{33,65},{65,33},{97,1},{2,98}... | collective-permute-start | bytes 1544 | tf_op jit(solution)/shard_map/ppermute | solution.py:39
  31.7 9.6 %collective-permute-start.6 = (bf16[640,512]{1,0:T(8,128)(2,1)S(1)}, bf16[640,512]{1,0:T(8,128)(2,1)S(1)}, u32[]{:S(2)}, u32[]{:S(2)}) collective-permute-start(bf16[640,512]{1,0:T(8,128)(2,1)S(1)} %collective-permute-done.5.refs_0_), channel_id=1, source_target_pairs={{0,1},{1,0},{2,3},{3,2},{4,5},{5,4},{6,7},{7,6},{8,9},{9,8},{10,11... | collective-permute-start | bytes 1966088 | tf_op jit(solution)/shard_map/ppermute | solution.py:35
  31.8 9.5 %collective-permute-start.8 = (bf16[640,512]{1,0:T(8,128)(2,1)S(1)}, bf16[640,512]{1,0:T(8,128)(2,1)S(1)}, u32[]{:S(2)}, u32[]{:S(2)}) collective-permute-start(bf16[640,512]{1,0:T(8,128)(2,1)S(1)} %collective-permute-done.7.refs_1_), channel_id=1, source_target_pairs={{0,1},{1,0},{2,3},{3,2},{4,5},{5,4},{6,7},{7,6},{8,9},{9,8},{10,11... | collective-permute-start | bytes 1966088 | tf_op jit(solution)/shard_map/ppermute | solution.py:35
  33.9 14.0 %collective-permute-start.4 = (bf16[640,512]{1,0:T(8,128)(2,1)S(1)}, bf16[640,512]{1,0:T(8,128)(2,1)S(1)}, u32[]{:S(2)}, u32[]{:S(2)}) collective-permute-start(bf16[640,512]{1,0:T(8,128)(2,1)S(1)} %collective-permute-done.3.refs_0_), channel_id=1, source_target_pairs={{0,1},{1,0},{2,3},{3,2},{4,5},{5,4},{6,7},{7,6},{8,9},{9,8},{10,11... | collective-permute-start | bytes 1966088 | tf_op jit(solution)/shard_map/ppermute | solution.py:35
  45.1 2.8 %copy-start.1 = (s32[512]{0:T(512)S(1)}, s32[512]{0:T(512)}, u32[]{:S(2)}) copy-start(s32[512]{0:T(512)} %param.10) | copy-start | bytes 6148
  48.0 8.2 %copy-start.5 = (s32[8]{0:T(128)S(1)}, s32[8]{0:T(128)}, u32[]{:S(2)}) copy-start(s32[8]{0:T(128)} %param.14) | copy-start | bytes 100
  48.0 23.2 %copy-start.3 = (f32[512]{0:T(512)S(1)}, f32[512]{0:T(512)}, u32[]{:S(2)}) copy-start(f32[512]{0:T(512)} %param.12) | copy-start | bytes 6148
  48.1 23.2 %copy-start.4 = (f32[512]{0:T(512)S(1)}, f32[512]{0:T(512)}, u32[]{:S(2)}) copy-start(f32[512]{0:T(512)} %param.11) | copy-start | bytes 6148
  52.9 8.9 %all-to-all-start = ((f32[8,4,512]{2,1,0:T(4,128)}), f32[8,4,512]{2,1,0:T(4,128)S(1)}, u32[]{:S(2)}, u32[]{:S(2)}) async-start(f32[8,4,512]{2,1,0:T(4,128)} %broadcast_in_dim.23), calls=%async_computation | async-start | bytes 131072 | tf_op jit(solution)/shard_map/all_to_all | solution.py:184
  62.5 8.7 %all-to-all-start.1 = ((f32[4,4,512]{2,1,0:T(4,128)}), f32[4,4,512]{2,1,0:T(4,128)S(1)}, u32[]{:S(2)}, u32[]{:S(2)}) async-start(f32[4,4,512]{2,1,0:T(4,128)} %broadcast_in_dim.24), calls=%async_computation.1 | async-start | bytes 65536 | tf_op jit(solution)/shard_map/all_to_all | solution.py:184
  65.8 17.9 %copy-start = (f32[512]{0:T(512)}, f32[512]{0:T(512)S(1)}, u32[]{:S(2)}) copy-start(f32[512]{0:T(512)S(1)} %select_reduce_fusion) | copy-start | bytes 6148
  73.1 3.6 %collective-permute-start.12 = (f32[1,128]{1,0:T(1,128)S(1)}, f32[1,128]{1,0:T(1,128)S(1)}, u32[]{:S(2)}, u32[]{:S(2)}) collective-permute-start(f32[1,128]{1,0:T(1,128)S(1)} %broadcast_in_dim.60), channel_id=1, source_target_pairs={{0,32},{32,0},{64,96},{96,64},{1,33},{33,1},{65,97},{97,65},{2,34}... | collective-permute-start | bytes 1544 | tf_op jit(solution)/shard_map/ppermute | solution.py:39
  77.4 4.9 %collective-permute-start.13 = (f32[1,128]{1,0:T(1,128)S(1)}, f32[1,128]{1,0:T(1,128)S(1)}, u32[]{:S(2)}, u32[]{:S(2)}) collective-permute-start(f32[1,128]{1,0:T(1,128)S(1)} %broadcast_add_fusion.1), channel_id=1, source_target_pairs={{0,96},{32,64},{64,32},{96,0},{1,97},{33,65},{65,33},{97,1},{2,98}... | collective-permute-start | bytes 1544 | tf_op jit(solution)/shard_map/ppermute | solution.py:39

commit v2 on v1

v2 whole, which is shorter than its diff:
```python
import functools

import jax
import jax.numpy as jnp
from jax import lax
from jax.experimental import pallas as pl
from jax.experimental.pallas import tpu as pltpu
from jax.sharding import PartitionSpec as P

GROUP = 8
LANES = 128
SIDE = 4
STEPS = (0, -1, 1, 2)
F32 = jnp.float32


def device(y, x, core):
    return ((y % SIDE) * SIDE + x % SIDE) * 2 + core


def everyone():
    return [(v // (2 * SIDE), v // 2 % SIDE, v % 2) for v in range(2 * SIDE * SIDE)]


def send_on(value, phase, step):
    pairs = []
    for y, x, core in everyone():
        to = (y, x + step, core) if core == phase else (y + step, x, core)
        pairs.append((device(y, x, core), device(*to)))
    return lax.ppermute(value, "vocab", pairs)


def swap(value):
    pairs = [(device(y, x, core), device(y, x, 1 - core)) for y, x, core in everyone()]
    return lax.ppermute(value, "vocab", pairs)


def block_rows(second, partner, depth):
    v = lax.axis_index("vocab")
    core = (v & 1) ^ partner
    x, y = (v >> 1) & (SIDE - 1), v >> 3
    rows = []
    for first in STEPS:
        dx = jnp.where(core == 0, first, second)
        dy = jnp.where(core == 0, second, first)
        block = (((y + dy) & (SIDE - 1)) * SIDE + ((x + dx) & (SIDE - 1))) * 2 + core
        rows.append(pl.multiple_of(block * depth, 32))
    return rows


def column_tiles(width):
    return [(b, min(b + 512, width)) for b in range(0, width, 512)]


def fetches(parts, depth, there, here, sems):
    rows = [r for part in parts for r in block_rows(*part, depth)]
    return [
        pltpu.make_async_copy(there.at[pl.ds(r, depth)], here.at[pl.ds(r, depth)], sems.at[k])
        for k, r in enumerate(rows)
    ]


def load_kernel(parts, depth, there, here, sems):
    copies = fetches(parts, depth, there, here, sems)
    for c in copies:
        c.start()
    for c in copies:
        c.wait()


def multiply(blocks, parts, depth, w_ref, acc_in, acc, lhs):
    rows, at = [], 0
    for ref, part in zip(blocks, parts):
        size = ref.shape[0]
        lhs[:, at : at + size] = ref[...].T
        rows += block_rows(*part, depth)
        at += size
    for b, e in column_tiles(w_ref.shape[1]):
        w = jnp.concatenate([w_ref[pl.ds(r, depth), b:e] for r in rows], axis=0)
        out = jnp.dot(lhs[...], w, preferred_element_type=F32)
        acc[:, b:e] = out if acc_in is None else acc_in[:, b:e] + out


def step_kernel(parts, later, depth, *refs):
    blocks, rest = refs[: len(parts)], refs[len(parts) :]
    w_ref, there = rest[:2]
    acc_in = rest[2] if len(rest) == 7 else None
    acc, here, lhs, sems = rest[-4:]
    copies = fetches(later, depth, there, here, sems)
    for c in copies:
        c.start()
    multiply(blocks, parts, depth, w_ref, acc_in, acc, lhs)
    for c in copies:
        c.wait()


def last_kernel(parts, depth, *refs):
    w_ref, acc_in, target, stats, acc, lhs = refs[len(parts) :]
    multiply(refs[: len(parts)], parts, depth, w_ref, acc_in, acc, lhs)
    tok, width = acc.shape
    step = 64
    tops, totals, moments, picks = [], [], [], []
    lane = lax.broadcasted_iota(jnp.int32, (step, LANES), 1) + lax.axis_index("vocab") * width
    for r in range(0, tok, step):
        want = target[r : r + step, :] - lane
        top = acc[r : r + step, 0:LANES]
        pick = jnp.where(want == 0, top, 0.0)
        for b in range(LANES, width, LANES):
            piece = acc[r : r + step, b : b + LANES]
            top = jnp.maximum(top, piece)
            pick = jnp.where(want == b, piece, pick)
        total = jnp.zeros_like(top)
        moment = jnp.zeros_like(top)
        for b in range(0, width, LANES):
            piece = acc[r : r + step, b : b + LANES]
            scaled = jnp.exp(piece - top)
            total += scaled
            moment += scaled * piece
        tops.append(top)
        totals.append(total)
        moments.append(moment)
        picks.append(pick)
    top, total, moment, pick = (
        jnp.concatenate(p, axis=0).T for p in (tops, totals, moments, picks)
    )
    best = jnp.max(top, axis=0, keepdims=True)
    scale = jnp.exp(top - best)
    mine = jnp.concatenate(
        [
            best,
            jnp.sum(total * scale, axis=0, keepdims=True),
            jnp.sum(moment * scale, axis=0, keepdims=True),
            jnp.sum(pick, axis=0, keepdims=True),
        ],
        axis=0,
    )
    for k in range(stats.shape[0]):
        stats[k] = mine


def in_vmem(value):
    return pltpu.with_memory_space_constraint(value, pltpu.VMEM)


def vmem_specs(count):
    return [pl.BlockSpec(memory_space=pltpu.VMEM)] * count


def in_hbm(value):
    return pltpu.with_memory_space_constraint(value, pltpu.HBM)


HBM_SPEC = pl.BlockSpec(memory_space=pltpu.HBM)
LIMIT = 16 << 20


def cost(flops):
    return pl.CostEstimate(flops=flops, bytes_accessed=1 << 20, transcendentals=0)


def load(weight, parts, depth):
    return pl.pallas_call(
        functools.partial(load_kernel, parts, depth),
        out_shape=pltpu.VMEM(weight.shape, weight.dtype),
        in_specs=[HBM_SPEC],
        out_specs=pl.BlockSpec(memory_space=pltpu.VMEM),
        scratch_shapes=[pltpu.SemaphoreType.DMA((SIDE * len(parts),))],
        cost_estimate=cost(1 << 31),
        compiler_params=pltpu.CompilerParams(vmem_limit_bytes=LIMIT),
    )(in_hbm(weight))


def product(blocks, parts, later, held, weight, acc):
    depth_sum = sum(b.shape[0] for b in blocks)
    rows, width = blocks[0].shape[1], weight.shape[1]
    depth = weight.shape[0] // lax.axis_size("vocab")
    operands = [*blocks, held] + ([] if acc is None else [acc])
    operands = [in_vmem(o) for o in operands]
    operands.insert(len(blocks) + 1, in_hbm(weight))
    specs = vmem_specs(len(operands))
    specs[len(blocks) + 1] = HBM_SPEC
    aliases = {len(blocks): 1} | ({} if acc is None else {len(blocks) + 2: 0})
    return pl.pallas_call(
        functools.partial(step_kernel, parts, later, depth),
        out_shape=(
            jax.ShapeDtypeStruct((rows, width), F32),
            jax.ShapeDtypeStruct(weight.shape, weight.dtype),
        ),
        in_specs=specs,
        out_specs=tuple(vmem_specs(2)),
        scratch_shapes=[
            pltpu.VMEM((rows, depth_sum), jnp.bfloat16),
            pltpu.SemaphoreType.DMA((SIDE * len(later),)),
        ],
        input_output_aliases=aliases,
        cost_estimate=cost(2 * rows * depth_sum * width),
        compiler_params=pltpu.CompilerParams(vmem_limit_bytes=LIMIT),
    )(*operands)


def statistics(blocks, parts, held, acc, target):
    depth_sum = sum(b.shape[0] for b in blocks)
    rows, width = acc.shape
    size = lax.axis_size("vocab")
    operands = (*blocks, held, acc, target)
    return pl.pallas_call(
        functools.partial(last_kernel, parts, held.shape[0] // size),
        out_shape=jax.ShapeDtypeStruct((size, 4, rows), F32),
        in_specs=vmem_specs(len(operands)),
        out_specs=pl.BlockSpec(memory_space=pltpu.VMEM),
        scratch_shapes=[
            pltpu.VMEM((rows, width), F32),
            pltpu.VMEM((rows, depth_sum), jnp.bfloat16),
        ],
        cost_estimate=cost(2 * rows * depth_sum * width),
        compiler_params=pltpu.CompilerParams(vmem_limit_bytes=LIMIT),
    )(*[in_vmem(o) for o in operands])


def own_rolls(rolls, tokens):
    token = lax.broadcasted_iota(jnp.int32, (rolls, tokens), 1)
    roll = lax.broadcasted_iota(jnp.int32, (rolls, tokens), 0)
    return token // (tokens // rolls) == roll, token % (tokens // rolls)


def as_columns(columns, base=None):
    lane = lax.broadcasted_iota(jnp.int32, (columns[0].shape[0], LANES), 1)
    out = jnp.zeros(lane.shape, F32) if base is None else base
    for k, column in enumerate(columns):
        out = jnp.where(lane == k, column, out)
    return out


def token_kernel(lines, old, ref, live, info, token_logprob, entropy, pack):
    count = lines.shape[0]
    top = lines[0, 0:1, :]
    for k in range(1, count):
        top = jnp.maximum(top, lines[k, 0:1, :])
    total, moment, pick = (jnp.zeros_like(top) for _ in range(3))
    for k in range(count):
        scale = jnp.exp(lines[k, 0:1, :] - top)
        total += lines[k, 1:2, :] * scale
        moment += lines[k, 2:3, :] * scale
        pick += lines[k, 3:4, :]
    lse = top + jnp.log(total)
    logprob = pick - lse
    spread = lse - moment / total
    token_logprob[...] = logprob
    entropy[...] = spread
    ratio = jnp.exp(jnp.clip(logprob - old[...], -20.0, 20.0))
    held = jnp.clip(ratio, 0.8, 1.2)
    shift = jnp.clip(ref[...] - logprob, -20.0, 20.0)
    divergence = jnp.exp(shift) - shift - 1.0
    mask = live[...]

    def of_rolls(row):
        return jnp.sum(mask * row, axis=1, keepdims=True)

    sums = [of_rolls(jnp.minimum(ratio, held)), of_rolls(jnp.maximum(ratio, held))]
    sums += [of_rolls(0.04 * divergence - 0.01 * spread), jnp.sum(mask, axis=1, keepdims=True)]
    pack[...] = as_columns(sums, info[...])


def loss_kernel(prompts, *refs):
    packs, (advantage, loss) = refs[:-2], refs[-2:]
    rolls = packs[0].shape[0]
    every = jnp.concatenate([p[...] for p in packs], axis=0)
    low, high, extra, count, score, prompt = (every[:, k : k + 1] for k in range(6))
    gain = jnp.zeros_like(score)
    for g in range(prompts):
        here = prompt == g
        mean = jnp.sum(jnp.where(here, score, 0.0), axis=0, keepdims=True) / GROUP
        square = jnp.sum(jnp.where(here, score * score, 0.0), axis=0, keepdims=True)
        spread = jnp.sqrt(jnp.maximum(square / GROUP - mean * mean, 0.0))
        gain = jnp.where(here, (score - mean) / jnp.maximum(spread, 1.0), gain)
    terms = extra - gain * jnp.where(gain >= 0.0, low, high)
    loss[...] = jnp.sum(terms, axis=0, keepdims=True) / jnp.sum(count, axis=0, keepdims=True)
    own, _ = own_rolls(rolls, advantage.shape[1])
    advantage[...] = jnp.sum(jnp.where(own, gain[:rolls], 0.0), axis=0, keepdims=True)


def small(kernel, operands, shapes):
    return pl.pallas_call(
        kernel,
        out_shape=tuple(jax.ShapeDtypeStruct(s, F32) for s in shapes),
        in_specs=vmem_specs(len(operands)),
        out_specs=tuple(vmem_specs(len(shapes))),
        compiler_params=pltpu.CompilerParams(vmem_limit_bytes=LIMIT),
    )(*[in_vmem(o) for o in operands])


def per_device(hidden, weight, targets, old_logprob, ref_logprob, lengths, rewards, group_ids):
    tok_rows, depth = hidden.shape
    line = [hidden.T]
    for step in (1, -1, 2):
        line.append(send_on(line[0], 0, step))
    sets = (
        ((0, 0), (0, 1)),
        ((-1, 0), (1, 0)),
        ((-1, 1), (1, 1)),
        ((2, 0), (2, 1)),
    )
    held = load(weight, sets[0], depth)
    line = jnp.concatenate(line, axis=0)
    line_p = swap(line)
    far, far_p = [], []
    for step in (1, -1, 2):
        far.append(send_on(line, 1, step))
    acc, held = product((line, line_p), sets[0], sets[1], held, weight, None)
    for k in range(3):
        far_p.append(swap(far[k]))
    acc, held = product(far[:2], sets[1], sets[2], held, weight, acc)
    acc, held = product(far_p[:2], sets[2], sets[3], held, weight, acc)
    target = jnp.broadcast_to(targets[:, None], (tok_rows, LANES))
    lines = statistics((far[2], far_p[2]), sets[3], held, acc, target)
    lines = lax.all_to_all(lines, "vocab", 0, 0, tiled=True)
    rolls = rewards.shape[0]
    own, position = own_rolls(rolls, tok_rows)
    live = (own & (position < lengths[:, None])).astype(F32)
    blank = jnp.zeros((rolls, 1), F32)
    info = as_columns(
        [blank] * 4 + [rewards.astype(F32)[:, None], group_ids.astype(F32)[:, None]]
    )
    row = (1, tok_rows)
    token_logprob, entropy, pack = small(
        token_kernel,
        (lines, old_logprob[None], ref_logprob[None], live, info),
        (row, row, (rolls, LANES)),
    )
    size = lax.axis_size("dp")
    packs = [
        lax.ppermute(pack, "dp", [(v, (v + step) % size) for v in range(size)])
        for step in range(1, size)
    ]
    advantage, loss = small(
        functools.partial(loss_kernel, rolls * size // GROUP), (pack, *packs), (row, (1, 1))
    )
    return (token_logprob[0], entropy[0], advantage[0], loss[0, 0])


def solution(mesh):
    return jax.shard_map(
        per_device,
        mesh=mesh,
        in_specs=(
            P("dp", "vocab"),
            P(None, "vocab"),
            P("dp"),
            P("dp"),
            P("dp"),
            P("dp"),
            P("dp"),
            P("dp"),
        ),
        out_specs=(P("dp"), P("dp"), P("dp"), P()),
        check_vma=False,
    )
```

time: 85.3 us -> 75 us (0.88)
  waiting for transfers between devices: 16 us -> 23.3 us
  other arithmetic: 8.8 us -> 2.44 us
  Pallas kernels: 27.4 us -> 21.8 us
  local copies, waits for them, and re-layouts: 2.7 us -> 0.15 us
  between operations: 2.8 us -> 0.78 us
  starting transfers between devices: 27.2 us -> 26.2 us
    ppermute x6, waiting for transfers between devices: 1.54 us -> 12.1 us  [send_on(): return lax.ppermute(value, 'vocab', pairs)]
    pallas_call x7, Pallas kernels: 27.4 us -> 21.8 us  [the longest x3 11.5 us: product(): pl.pallas_call(functools.partial(step_kernel, parts, later, depth), out_s...]
    reduce_sum x7 -> x0, other arithmetic: 3.55 us -> none  [the longest x1 1.33 us: per_device(): mask = jnp.sum(live.astype(F32), axis=0)]
    ppermute x4, starting transfers between devices: 0.63 us -> 3.64 us  [swap(): return lax.ppermute(value, 'vocab', pairs)]
    ppermute x4 -> x3, starting transfers between devices: 9.34 us -> 6.52 us  [per_device(): lax.ppermute(pack, 'dp', [(v, (v + step) % size) for v in range(size)])]
    all_to_all x2 -> x1, waiting for transfers between devices: 10.9 us -> 8.68 us  [per_device(): lines = lax.all_to_all(lines, 'vocab', 0, 0, tiled=True)]
    add x5 -> x1, other arithmetic: 2.03 us -> 0.01 us  [own_rolls(): return (token // (tokens // rolls) == roll, token % (tokens // rolls))]
    broadcast_in_dim x5 -> x1, local copies, waits for them, and re-layouts: 2.01 us -> 0.12 us  [per_device(): target = jnp.broadcast_to(targets[:, None], (tok_rows, LANES))]
  transfers between devices with their start and end apart: 16 -> 14, of which waited for: 5 -> 9; matrix products, arithmetic and copies ran while one was open for 8% -> 2% of each run, Pallas kernels for 27% -> 19%
where the time goes in v2:
time: 75 us; the launch traced here: 74.7 us
  starting transfers between devices  26.2 us (35%)
  waiting for transfers between devices  23.3 us (31%)
  Pallas kernels  21.8 us (29%)
  other arithmetic  2.44 us (3%)
  between operations  0.78 us (1%)
    ppermute x6, waiting for transfers between devices, send_on(): return lax.ppermute(value, 'vocab', pairs)  12.1 us
    pallas_call x3, Pallas kernels, product(): pl.pallas_call(functools.partial(step_kernel, parts, later, depth), out_s...  11.5 us
    ppermute x6, starting transfers between devices, send_on(): return lax.ppermute(value, 'vocab', pairs)  10.6 us
    all_to_all x1, waiting for transfers between devices, per_device(): lines = lax.all_to_all(lines, 'vocab', 0, 0, tiled=True)  8.68 us
    ppermute x3, starting transfers between devices, per_device(): lax.ppermute(pack, 'dp', [(v, (v + step) % size) for v in range(size)])  6.52 us
    pallas_call x1, Pallas kernels, statistics(): pl.pallas_call(functools.partial(last_kernel, parts, held.shape[0] // siz...  5.83 us
    all_to_all x1, starting transfers between devices, per_device(): lines = lax.all_to_all(lines, 'vocab', 0, 0, tiled=True)  5.43 us
    ppermute x4, starting transfers between devices, swap(): return lax.ppermute(value, 'vocab', pairs)  3.64 us
  transfers between devices with their start and end apart: 14, of which 9 were waited for; matrix products, arithmetic and copies ran while one was open for 2% of the time, Pallas kernels for 19%

profile of v2, /device:TPU:0, one launch (start us, length us, event | category | flops | bytes accessed | tf_op | source)
XLA Modules:
  0.0 74.7 jit_solution(2927765385157494146)
XLA Ops:
  0.6 1.7 %collective-permute-start = (bf16[160,512]{1,0:T(8,128)(2,1)}, bf16[160,512]{1,0:T(8,128)(2,1)S(1)}, u32[]{:S(2)}, u32[]{:S(2)}) collective-permute-start(bf16[160,512]{1,0:T(8,128)(2,1)} %bitcast.9), channel_id=1, source_target_pairs={{0,2},{1,9},{2,4},{3,11},{4,6},{5,13},{6,0},{7,15},{8,10},{9,17},{... | collective-permute-start | bytes 491528 | tf_op jit(solution)/shard_map/ppermute | solution.py:30
  2.3 1.6 %collective-permute-start.1 = (bf16[160,512]{1,0:T(8,128)(2,1)}, bf16[160,512]{1,0:T(8,128)(2,1)S(1)}, u32[]{:S(2)}, u32[]{:S(2)}) collective-permute-start(bf16[160,512]{1,0:T(8,128)(2,1)} %bitcast.10), channel_id=1, source_target_pairs={{0,6},{1,25},{2,0},{3,27},{4,2},{5,29},{6,4},{7,31},{8,14},{9,1},{... | collective-permute-start | bytes 491528 | tf_op jit(solution)/shard_map/ppermute | solution.py:30
  3.9 1.9 %collective-permute-start.2 = (bf16[160,512]{1,0:T(8,128)(2,1)}, bf16[160,512]{1,0:T(8,128)(2,1)S(1)}, u32[]{:S(2)}, u32[]{:S(2)}) collective-permute-start(bf16[160,512]{1,0:T(8,128)(2,1)} %bitcast.11), channel_id=1, source_target_pairs={{0,4},{1,17},{2,6},{3,19},{4,0},{5,21},{6,2},{7,23},{8,12},{9,25},... | collective-permute-start | bytes 491528 | tf_op jit(solution)/shard_map/ppermute | solution.py:30
  5.9 1.6 %collective-permute-done = bf16[160,512]{1,0:T(8,128)(2,1)S(1)} collective-permute-done((bf16[160,512]{1,0:T(8,128)(2,1)}, bf16[160,512]{1,0:T(8,128)(2,1)S(1)}, u32[]{:S(2)}, u32[]{:S(2)}) %collective-permute-start) | collective-permute-done | bytes 163872 | tf_op jit(solution)/shard_map/ppermute | solution.py:30
  7.4 0.4 collective-permute-done.1
  7.8 3.1 %collective-permute-done.2 = bf16[160,512]{1,0:T(8,128)(2,1)S(1)} collective-permute-done((bf16[160,512]{1,0:T(8,128)(2,1)}, bf16[160,512]{1,0:T(8,128)(2,1)S(1)}, u32[]{:S(2)}, u32[]{:S(2)}) %collective-permute-start.2) | collective-permute-done | bytes 163872 | tf_op jit(solution)/shard_map/ppermute | solution.py:30
  11.0 1.0 %pad_maximum_fusion.refs_0_ = bf16[640,512]{1,0:T(8,128)(2,1)S(1)} fusion(bf16[160,512]{1,0:T(8,128)(2,1)S(1)} %collective-permute-done.2, bf16[160,512]{1,0:T(8,128)(2,1)S(1)} %collective-permute-done.1, bf16[160,512]{1,0:T(8,128)(2,1)S(1)} %collective-permute-done, bf16[160,512]{1,0:T(8,128)(2,1)} %bitcast.12), kind=kLoop, calls=%fused_computation | loop fusion | flops 2621440 | bytes 1310720 | tf_op jit(solution)/shard_map/concatenate | solution.py:304
  11.9 1.8 %collective-permute-start.5 = (bf16[640,512]{1,0:T(8,128)(2,1)S(1)}, bf16[640,512]{1,0:T(8,128)(2,1)S(1)}, u32[]{:S(2)}, u32[]{:S(2)}) collective-permute-start(bf16[640,512]{1,0:T(8,128)(2,1)S(1)} %pad_maximum_fusion.refs_0_), channel_id=1, source_target_pairs={{0,8},{1,3},{2,10},{3,5},{4,12},{5,7},{6,14},{7,1},{8,16},{9,11},{... | collective-permute-start | bytes 1966088 | tf_op jit(solution)/shard_map/ppermute | solution.py:30
  13.7 1.5 %collective-permute-start.7 = (bf16[640,512]{1,0:T(8,128)(2,1)S(1)}, bf16[640,512]{1,0:T(8,128)(2,1)S(1)}, u32[]{:S(2)}, u32[]{:S(2)}) collective-permute-start(bf16[640,512]{1,0:T(8,128)(2,1)S(1)} %pad_maximum_fusion.refs_0_), channel_id=1, source_target_pairs={{0,24},{1,7},{2,26},{3,1},{4,28},{5,3},{6,30},{7,5},{8,0},{9,15},{... | collective-permute-start | bytes 1966088 | tf_op jit(solution)/shard_map/ppermute | solution.py:30
  15.2 0.0 collective-permute-start.9
  15.2 2.1 %collective-permute-start.3 = (bf16[640,512]{1,0:T(8,128)(2,1)S(1)}, bf16[640,512]{1,0:T(8,128)(2,1)S(1)}, u32[]{:S(2)}, u32[]{:S(2)}) collective-permute-start(bf16[640,512]{1,0:T(8,128)(2,1)S(1)} %pad_maximum_fusion.refs_0_), channel_id=1, source_target_pairs={{0,16},{1,5},{2,18},{3,7},{4,20},{5,1},{6,22},{7,3},{8,24},{9,13},... | collective-permute-start | bytes 1966088 | tf_op jit(solution)/shard_map/ppermute | solution.py:30
  17.3 0.7 convert_element_type.10
  18.0 0.7 convert_element_type.11
  18.7 2.8 %shard_map.111.refs_2_ = bf16[5120,2432]{1,0:T(8,128)(2,1)S(1)} custom-call(bf16[5120,2432]{1,0:T(8,128)(2,1)} %refs_3_.5), custom_call_target="tpu_custom_call" | custom-call | flops 2147483648 | bytes 1048576 | tf_op jit(solution)/shard_map/pallas_call | solution.py:162
  21.5 0.1 select_select_fusion.info
  21.6 2.2 %collective-permute-done.5.refs_0_ = bf16[640,512]{1,0:T(8,128)(2,1)S(1)} collective-permute-done((bf16[640,512]{1,0:T(8,128)(2,1)S(1)}, bf16[640,512]{1,0:T(8,128)(2,1)S(1)}, u32[]{:S(2)}, u32[]{:S(2)}) %collective-permute-start.5) | collective-permute-done | bytes 655392 | tf_op jit(solution)/shard_map/ppermute | solution.py:30
  23.8 0.0 collective-permute-start.6
  23.8 0.5 collective-permute-done.7.refs_1_
  24.3 3.6 %collective-permute-start.8 = (bf16[640,512]{1,0:T(8,128)(2,1)S(1)}, bf16[640,512]{1,0:T(8,128)(2,1)S(1)}, u32[]{:S(2)}, u32[]{:S(2)}) collective-permute-start(bf16[640,512]{1,0:T(8,128)(2,1)S(1)} %collective-permute-done.7.refs_1_), channel_id=1, source_target_pairs={{0,1},{1,0},{2,3},{3,2},{4,5},{5,4},{6,7},{7,6},{8,9},{9,8},{10,11... | collective-permute-start | bytes 1966088 | tf_op jit(solution)/shard_map/ppermute | solution.py:35
  27.9 4.3 %collective-permute-done.3.refs_0_ = bf16[640,512]{1,0:T(8,128)(2,1)S(1)} collective-permute-done((bf16[640,512]{1,0:T(8,128)(2,1)S(1)}, bf16[640,512]{1,0:T(8,128)(2,1)S(1)}, u32[]{:S(2)}, u32[]{:S(2)}) %collective-permute-start.3) | collective-permute-done | bytes 655392 | tf_op jit(solution)/shard_map/ppermute | solution.py:30
  32.2 0.0 collective-permute-start.4
  32.2 0.0 collective-permute-done.9.refs_1_
  32.2 3.7 %shard_map.112 = (f32[512,2432]{1,0:T(8,128)S(1)}, bf16[5120,2432]{1,0:T(8,128)(2,1)S(1)}) custom-call(bf16[640,512]{1,0:T(8,128)(2,1)S(1)} %pad_maximum_fusion.refs_0_, bf16[640,512]{1,0:T(8,128)(2,1)S(1)} %collective-permute-done.9.refs_1_, bf16[5120,2432]{1,0:T(8,128)(2,1)S(1)} %shard_map.111.refs_2_, ...), custom_call_target="tpu_custom_call", output_to_operand_aliasing={{1}: (2, {})} | custom-call | flops 3187671040 | bytes 1048576 | tf_op jit(solution)/shard_map/pallas_call | solution.py:183
  35.9 3.9 %shard_map.113 = (f32[512,2432]{1,0:T(8,128)S(1)}, bf16[5120,2432]{1,0:T(8,128)(2,1)S(1)}) custom-call(bf16[640,512]{1,0:T(8,128)(2,1)S(1)} %collective-permute-done.5.refs_0_, bf16[640,512]{1,0:T(8,128)(2,1)S(1)} %collective-permute-done.7.refs_1_, bf16[5120,2432]{1,0:T(8,128)(2,1)S(1)} %get-tuple-element.15.refs_2_, ...), custom_call_target="tpu_custom_call", output_to_operand_aliasing={{1}: (2, {}), {0}: (4, {})} | custom-call | flops 3187671040 | bytes 1048576 | tf_op jit(solution)/shard_map/pallas_call | solution.py:183
  39.8 0.0 collective-permute-done.6.refs_0_
  39.8 0.0 collective-permute-done.8.refs_1_
  39.8 0.0 copy-start.2
  39.8 3.9 %shard_map.114 = (f32[512,2432]{1,0:T(8,128)S(1)}, bf16[5120,2432]{1,0:T(8,128)(2,1)S(1)}) custom-call(bf16[640,512]{1,0:T(8,128)(2,1)S(1)} %collective-permute-done.6.refs_0_, bf16[640,512]{1,0:T(8,128)(2,1)S(1)} %collective-permute-done.8.refs_1_, bf16[5120,2432]{1,0:T(8,128)(2,1)S(1)} %get-tuple-element.17.refs_2_, ...), custom_call_target="tpu_custom_call", output_to_operand_aliasing={{1}: (2, {}), {0}: (4, {})} | custom-call | flops 3187671040 | bytes 1048576 | tf_op jit(solution)/shard_map/pallas_call | solution.py:183
  43.8 0.0 collective-permute-done.4.refs_1_
  43.8 0.0 copy-done.2
  43.8 0.1 broadcast_in_dim.41.refs_4_
  43.9 0.0 copy-start.3
  43.9 0.0 copy-start
  44.0 0.0 copy-start.1
  44.0 5.8 %shard_map.115 = f32[32,4,512]{2,1,0:T(4,128)} custom-call(bf16[640,512]{1,0:T(8,128)(2,1)S(1)} %collective-permute-done.3.refs_0_, bf16[640,512]{1,0:T(8,128)(2,1)S(1)} %collective-permute-done.4.refs_1_, bf16[5120,2432]{1,0:T(8,128)(2,1)S(1)} %get-tuple-element.19.refs_2_, f32[512,2432]{1,0:T(8,128)S(1)} %get-tuple-element.20.refs_3_, ...), custom_call_target="tpu_custom_call" | custom-call | flops 3187671040 | bytes 1048576 | tf_op jit(solution)/shard_map/pallas_call | solution.py:206
  49.8 5.4 %all-to-all-start = ((f32[32,4,512]{2,1,0:T(4,128)}), f32[32,4,512]{2,1,0:T(4,128)S(1)}, u32[]{:S(2)}, u32[]{:S(2)}) async-start(f32[32,4,512]{2,1,0:T(4,128)} %shard_map.115), calls=%async_computation | async-start | bytes 524288 | tf_op jit(solution)/shard_map/all_to_all | solution.py:316
  55.3 0.0 copy-done.3
  55.3 0.1 fusion.1.live
  55.3 8.7 %all-to-all-done.lines = f32[32,4,512]{2,1,0:T(4,128)S(1)} async-done(((f32[32,4,512]{2,1,0:T(4,128)}), f32[32,4,512]{2,1,0:T(4,128)S(1)}, u32[]{:S(2)}, u32[]{:S(2)}) %all-to-all-start) | async-done | bytes 262176 | tf_op jit(solution)/shard_map/all_to_all | solution.py:316
  64.0 0.0 copy-done
  64.0 0.0 copy-done.1
  64.0 0.7 shard_map.116
  64.7 1.9 %collective-permute-start.10 = (f32[8,128]{1,0:T(8,128)S(1)}, f32[8,128]{1,0:T(8,128)S(1)}, u32[]{:S(2)}, u32[]{:S(2)}) collective-permute-start(f32[8,128]{1,0:T(8,128)S(1)} %get-tuple-element.23.refs_0_), channel_id=1, source_target_pairs={{0,32},{32,64},{64,96},{96,0},{1,33},{33,65},{65,97},{97,1},{2,34}... | collective-permute-start | bytes 12296 | tf_op jit(solution)/shard_map/ppermute | solution.py:332
  66.6 3.6 %collective-permute-start.11 = (f32[8,128]{1,0:T(8,128)S(1)}, f32[8,128]{1,0:T(8,128)S(1)}, u32[]{:S(2)}, u32[]{:S(2)}) collective-permute-start(f32[8,128]{1,0:T(8,128)S(1)} %get-tuple-element.23.refs_0_), channel_id=1, source_target_pairs={{0,64},{32,96},{64,0},{96,32},{1,65},{33,97},{65,1},{97,33},{2,66}... | collective-permute-start | bytes 12296 | tf_op jit(solution)/shard_map/ppermute | solution.py:332
  70.2 1.0 %collective-permute-start.12 = (f32[8,128]{1,0:T(8,128)S(1)}, f32[8,128]{1,0:T(8,128)S(1)}, u32[]{:S(2)}, u32[]{:S(2)}) collective-permute-start(f32[8,128]{1,0:T(8,128)S(1)} %get-tuple-element.23.refs_0_), channel_id=1, source_target_pairs={{0,96},{32,0},{64,32},{96,64},{1,97},{33,1},{65,33},{97,65},{2,98}... | collective-permute-start | bytes 12296 | tf_op jit(solution)/shard_map/ppermute | solution.py:332
  71.2 0.0 collective-permute-done.10.refs_1_
  71.2 0.6 collective-permute-done.11.refs_2_
  71.8 2.0 %collective-permute-done.12.refs_3_ = f32[8,128]{1,0:T(8,128)S(1)} collective-permute-done((f32[8,128]{1,0:T(8,128)S(1)}, f32[8,128]{1,0:T(8,128)S(1)}, u32[]{:S(2)}, u32[]{:S(2)}) %collective-permute-start.12) | collective-permute-done | bytes 4128 | tf_op jit(solution)/shard_map/ppermute | solution.py:332
  73.8 0.9 %shard_map.117 = (f32[1,512]{1,0:T(1,128)}, f32[1,1]{1,0:T(1,128)}) custom-call(f32[8,128]{1,0:T(8,128)S(1)} %get-tuple-element.23.refs_0_, f32[8,128]{1,0:T(8,128)S(1)} %collective-permute-done.10.refs_1_, f32[8,128]{1,0:T(8,128)S(1)} %collective-permute-done.11.refs_2_, f32[8,128]{1,0:T(8,128)S(1)} %collective-permute-done.12.refs_3_), custom_call_target="tpu_custom_call" | custom-call | tf_op jit(solution)/shard_map/pallas_call | solution.py:283
  (4 shorter events, 0.0 us)
Async XLA Ops:
  0.6 6.8 %collective-permute-start = (bf16[160,512]{1,0:T(8,128)(2,1)}, bf16[160,512]{1,0:T(8,128)(2,1)S(1)}, u32[]{:S(2)}, u32[]{:S(2)}) collective-permute-start(bf16[160,512]{1,0:T(8,128)(2,1)} %bitcast.9), channel_id=1, source_target_pairs={{0,2},{1,9},{2,4},{3,11},{4,6},{5,13},{6,0},{7,15},{8,10},{9,17},{... | collective-permute-start | bytes 491528 | tf_op jit(solution)/shard_map/ppermute | solution.py:30
  2.3 5.5 %collective-permute-start.1 = (bf16[160,512]{1,0:T(8,128)(2,1)}, bf16[160,512]{1,0:T(8,128)(2,1)S(1)}, u32[]{:S(2)}, u32[]{:S(2)}) collective-permute-start(bf16[160,512]{1,0:T(8,128)(2,1)} %bitcast.10), channel_id=1, source_target_pairs={{0,6},{1,25},{2,0},{3,27},{4,2},{5,29},{6,4},{7,31},{8,14},{9,1},{... | collective-permute-start | bytes 491528 | tf_op jit(solution)/shard_map/ppermute | solution.py:30
  3.9 7.0 %collective-permute-start.2 = (bf16[160,512]{1,0:T(8,128)(2,1)}, bf16[160,512]{1,0:T(8,128)(2,1)S(1)}, u32[]{:S(2)}, u32[]{:S(2)}) collective-permute-start(bf16[160,512]{1,0:T(8,128)(2,1)} %bitcast.11), channel_id=1, source_target_pairs={{0,4},{1,17},{2,6},{3,19},{4,0},{5,21},{6,2},{7,23},{8,12},{9,25},... | collective-permute-start | bytes 491528 | tf_op jit(solution)/shard_map/ppermute | solution.py:30
  11.9 11.9 %collective-permute-start.5 = (bf16[640,512]{1,0:T(8,128)(2,1)S(1)}, bf16[640,512]{1,0:T(8,128)(2,1)S(1)}, u32[]{:S(2)}, u32[]{:S(2)}) collective-permute-start(bf16[640,512]{1,0:T(8,128)(2,1)S(1)} %pad_maximum_fusion.refs_0_), channel_id=1, source_target_pairs={{0,8},{1,3},{2,10},{3,5},{4,12},{5,7},{6,14},{7,1},{8,16},{9,11},{... | collective-permute-start | bytes 1966088 | tf_op jit(solution)/shard_map/ppermute | solution.py:30
  13.7 10.6 %collective-permute-start.7 = (bf16[640,512]{1,0:T(8,128)(2,1)S(1)}, bf16[640,512]{1,0:T(8,128)(2,1)S(1)}, u32[]{:S(2)}, u32[]{:S(2)}) collective-permute-start(bf16[640,512]{1,0:T(8,128)(2,1)S(1)} %pad_maximum_fusion.refs_0_), channel_id=1, source_target_pairs={{0,24},{1,7},{2,26},{3,1},{4,28},{5,3},{6,30},{7,5},{8,0},{9,15},{... | collective-permute-start | bytes 1966088 | tf_op jit(solution)/shard_map/ppermute | solution.py:30
  15.2 16.9 %collective-permute-start.9 = (bf16[640,512]{1,0:T(8,128)(2,1)S(1)}, bf16[640,512]{1,0:T(8,128)(2,1)S(1)}, u32[]{:S(2)}, u32[]{:S(2)}) collective-permute-start(bf16[640,512]{1,0:T(8,128)(2,1)S(1)} %pad_maximum_fusion.refs_0_), channel_id=1, source_target_pairs={{0,1},{1,0},{2,3},{3,2},{4,5},{5,4},{6,7},{7,6},{8,9},{9,8},{10,11... | collective-permute-start | bytes 1966088 | tf_op jit(solution)/shard_map/ppermute | solution.py:35
  15.2 16.9 %collective-permute-start.3 = (bf16[640,512]{1,0:T(8,128)(2,1)S(1)}, bf16[640,512]{1,0:T(8,128)(2,1)S(1)}, u32[]{:S(2)}, u32[]{:S(2)}) collective-permute-start(bf16[640,512]{1,0:T(8,128)(2,1)S(1)} %pad_maximum_fusion.refs_0_), channel_id=1, source_target_pairs={{0,16},{1,5},{2,18},{3,7},{4,20},{5,1},{6,22},{7,3},{8,24},{9,13},... | collective-permute-start | bytes 1966088 | tf_op jit(solution)/shard_map/ppermute | solution.py:30
  23.8 16.0 %collective-permute-start.6 = (bf16[640,512]{1,0:T(8,128)(2,1)S(1)}, bf16[640,512]{1,0:T(8,128)(2,1)S(1)}, u32[]{:S(2)}, u32[]{:S(2)}) collective-permute-start(bf16[640,512]{1,0:T(8,128)(2,1)S(1)} %collective-permute-done.5.refs_0_), channel_id=1, source_target_pairs={{0,1},{1,0},{2,3},{3,2},{4,5},{5,4},{6,7},{7,6},{8,9},{9,8},{10,11... | collective-permute-start | bytes 1966088 | tf_op jit(solution)/shard_map/ppermute | solution.py:35
  24.3 15.5 %collective-permute-start.8 = (bf16[640,512]{1,0:T(8,128)(2,1)S(1)}, bf16[640,512]{1,0:T(8,128)(2,1)S(1)}, u32[]{:S(2)}, u32[]{:S(2)}) collective-permute-start(bf16[640,512]{1,0:T(8,128)(2,1)S(1)} %collective-permute-done.7.refs_1_), channel_id=1, source_target_pairs={{0,1},{1,0},{2,3},{3,2},{4,5},{5,4},{6,7},{7,6},{8,9},{9,8},{10,11... | collective-permute-start | bytes 1966088 | tf_op jit(solution)/shard_map/ppermute | solution.py:35
  32.2 11.6 %collective-permute-start.4 = (bf16[640,512]{1,0:T(8,128)(2,1)S(1)}, bf16[640,512]{1,0:T(8,128)(2,1)S(1)}, u32[]{:S(2)}, u32[]{:S(2)}) collective-permute-start(bf16[640,512]{1,0:T(8,128)(2,1)S(1)} %collective-permute-done.3.refs_0_), channel_id=1, source_target_pairs={{0,1},{1,0},{2,3},{3,2},{4,5},{5,4},{6,7},{7,6},{8,9},{9,8},{10,11... | collective-permute-start | bytes 1966088 | tf_op jit(solution)/shard_map/ppermute | solution.py:35
  39.8 4.0 %copy-start.2 = (s32[512]{0:T(512)S(1)}, s32[512]{0:T(512)}, u32[]{:S(2)}) copy-start(s32[512]{0:T(512)} %param.10) | copy-start | bytes 6148
  43.9 11.3 %copy-start.3 = (s32[8]{0:T(128)S(1)}, s32[8]{0:T(128)}, u32[]{:S(2)}) copy-start(s32[8]{0:T(128)} %param.13) | copy-start | bytes 100
  43.9 20.1 %copy-start = (f32[512]{0:T(512)S(1)}, f32[512]{0:T(512)}, u32[]{:S(2)}) copy-start(f32[512]{0:T(512)} %param.11) | copy-start | bytes 6148
  44.0 20.1 %copy-start.1 = (f32[512]{0:T(512)S(1)}, f32[512]{0:T(512)}, u32[]{:S(2)}) copy-start(f32[512]{0:T(512)} %param.12) | copy-start | bytes 6148
  49.8 14.2 %all-to-all-start = ((f32[32,4,512]{2,1,0:T(4,128)}), f32[32,4,512]{2,1,0:T(4,128)S(1)}, u32[]{:S(2)}, u32[]{:S(2)}) async-start(f32[32,4,512]{2,1,0:T(4,128)} %shard_map.115), calls=%async_computation | async-start | bytes 524288 | tf_op jit(solution)/shard_map/all_to_all | solution.py:316
  64.7 6.5 %collective-permute-start.10 = (f32[8,128]{1,0:T(8,128)S(1)}, f32[8,128]{1,0:T(8,128)S(1)}, u32[]{:S(2)}, u32[]{:S(2)}) collective-permute-start(f32[8,128]{1,0:T(8,128)S(1)} %get-tuple-element.23.refs_0_), channel_id=1, source_target_pairs={{0,32},{32,64},{64,96},{96,0},{1,33},{33,65},{65,97},{97,1},{2,34}... | collective-permute-start | bytes 12296 | tf_op jit(solution)/shard_map/ppermute | solution.py:332
  66.6 5.2 %collective-permute-start.11 = (f32[8,128]{1,0:T(8,128)S(1)}, f32[8,128]{1,0:T(8,128)S(1)}, u32[]{:S(2)}, u32[]{:S(2)}) collective-permute-start(f32[8,128]{1,0:T(8,128)S(1)} %get-tuple-element.23.refs_0_), channel_id=1, source_target_pairs={{0,64},{32,96},{64,0},{96,32},{1,65},{33,97},{65,1},{97,33},{2,66}... | collective-permute-start | bytes 12296 | tf_op jit(solution)/shard_map/ppermute | solution.py:332
  70.2 3.6 %collective-permute-start.12 = (f32[8,128]{1,0:T(8,128)S(1)}, f32[8,128]{1,0:T(8,128)S(1)}, u32[]{:S(2)}, u32[]{:S(2)}) collective-permute-start(f32[8,128]{1,0:T(8,128)S(1)} %get-tuple-element.23.refs_0_), channel_id=1, source_target_pairs={{0,96},{32,0},{64,32},{96,64},{1,97},{33,1},{65,33},{97,65},{2,98}... | collective-permute-start | bytes 12296 | tf_op jit(solution)/shard_map/ppermute | solution.py:332

commit v3 on v2

--- a/solution.py
+++ b/solution.py
@@ -35,17 +35,29 @@
     return lax.ppermute(value, "vocab", pairs)
 
 
-def block_rows(second, partner, depth):
+def block_rows(blocks, partner, depth):
     v = lax.axis_index("vocab")
     core = (v & 1) ^ partner
     x, y = (v >> 1) & (SIDE - 1), v >> 3
     rows = []
-    for first in STEPS:
+    for first, second in blocks:
         dx = jnp.where(core == 0, first, second)
         dy = jnp.where(core == 0, second, first)
         block = (((y + dy) & (SIDE - 1)) * SIDE + ((x + dx) & (SIDE - 1))) * 2 + core
         rows.append(pl.multiple_of(block * depth, 32))
     return rows
+
+
+LINE = tuple((first, 0) for first in STEPS)
+SIDES = ((0, -1), (0, 1))
+
+
+def far_blocks(second, steps=STEPS):
+    return tuple((first, second) for first in steps)
+
+
+def padded(size):
+    return -(-size // 256) * 256
 
 
 def column_tiles(width):
@@ -68,17 +80,29 @@
         c.wait()
 
 
-def multiply(blocks, parts, depth, w_ref, acc_in, acc, lhs):
-    rows, at = [], 0
-    for ref, part in zip(blocks, parts):
+def rows_between(refs, lo, hi):
+    pieces, at = [], 0
+    for ref in refs:
         size = ref.shape[0]
-        lhs[:, at : at + size] = ref[...].T
-        rows += block_rows(*part, depth)
+        b, e = max(lo - at, 0), min(hi - at, size)
+        if b < e:
+            pieces.append(ref[b:e, :])
         at += size
+    if at < hi:
+        pieces.append(jnp.zeros((hi - max(lo, at), refs[0].shape[1]), refs[0].dtype))
+    return jnp.concatenate(pieces, axis=0) if len(pieces) > 1 else pieces[0]
+
+
+def multiply(blocks, parts, depth, w_ref, lhs, emit):
+    rows = [r for part in parts for r in block_rows(*part, depth)]
+    extra = lhs.shape[1] - len(rows) * depth
+    for k in range(0, lhs.shape[1], 256):
+        lhs[:, k : k + 256] = rows_between(blocks, k, k + 256).T
     for b, e in column_tiles(w_ref.shape[1]):
-        w = jnp.concatenate([w_ref[pl.ds(r, depth), b:e] for r in rows], axis=0)
-        out = jnp.dot(lhs[...], w, preferred_element_type=F32)
-        acc[:, b:e] = out if acc_in is None else acc_in[:, b:e] + out
+        w = [w_ref[pl.ds(r, depth), b:e] for r in rows]
+        if extra:
+            w.append(w_ref[pl.ds(rows[0], extra), b:e])
+        emit(b, e, jnp.dot(lhs[...], jnp.concatenate(w, axis=0), preferred_element_type=F32))
 
 
 def step_kernel(parts, later, depth, *refs):
@@ -89,26 +113,38 @@
     copies = fetches(later, depth, there, here, sems)
     for c in copies:
         c.start()
-    multiply(blocks, parts, depth, w_ref, acc_in, acc, lhs)
+
+    def emit(b, e, out):
+        acc[:, b:e] = out if acc_in is None else acc_in[:, b:e] + out
+
+    multiply(blocks, parts, depth, w_ref, lhs, emit)
     for c in copies:
         c.wait()
 
 
 def last_kernel(parts, depth, *refs):
-    w_ref, acc_in, target, stats, acc, lhs = refs[len(parts) :]
-    multiply(refs[: len(parts)], parts, depth, w_ref, acc_in, acc, lhs)
+    w_ref, acc_in, target, stats, acc, tops, picks, lhs = refs[len(parts) :]
     tok, width = acc.shape
     step = 64
-    tops, totals, moments, picks = [], [], [], []
-    lane = lax.broadcasted_iota(jnp.int32, (step, LANES), 1) + lax.axis_index("vocab") * width
+    first = lax.axis_index("vocab") * width
+    lane = lax.broadcasted_iota(jnp.int32, (tok, LANES), 1) + first
+
+    def emit(b, e, out):
+        new = acc_in[:, b:e] + out
+        acc[:, b:e] = new
+        pieces = [new[:, k : k + LANES] for k in range(0, e - b, LANES)]
+        top = functools.reduce(jnp.maximum, pieces)
+        want = target[...] - lane
+        pick = jnp.zeros_like(top) if b == 0 else picks[...]
+        for k, piece in enumerate(pieces):
+            pick = jnp.where(want == b + k * LANES, piece, pick)
+        tops[...] = top if b == 0 else jnp.maximum(tops[...], top)
+        picks[...] = pick
+
+    multiply(refs[: len(parts)], parts, depth, w_ref, lhs, emit)
+    totals, moments = [], []
     for r in range(0, tok, step):
-        want = target[r : r + step, :] - lane
-        top = acc[r : r + step, 0:LANES]
-        pick = jnp.where(want == 0, top, 0.0)
-        for b in range(LANES, width, LANES):
-            piece = acc[r : r + step, b : b + LANES]
-            top = jnp.maximum(top, piece)
-            pick = jnp.where(want == b, piece, pick)
+        top = tops[r : r + step, :]
         total = jnp.zeros_like(top)
         moment = jnp.zeros_like(top)
         for b in range(0, width, LANES):
@@ -116,13 +152,10 @@
             scaled = jnp.exp(piece - top)
             total += scaled
             moment += scaled * piece
-        tops.append(top)
         totals.append(total)
         moments.append(moment)
-        picks.append(pick)
-    top, total, moment, pick = (
-        jnp.concatenate(p, axis=0).T for p in (tops, totals, moments, picks)
-    )
+    total, moment = (jnp.concatenate(p, axis=0).T for p in (totals, moments))
+    top, pick = tops[...].T, picks[...].T
     best = jnp.max(top, axis=0, keepdims=True)
     scale = jnp.exp(top - best)
     mine = jnp.concatenate(
@@ -158,13 +191,17 @@
     return pl.CostEstimate(flops=flops, bytes_accessed=1 << 20, transcendentals=0)
 
 
+def count_of(parts):
+    return sum(len(blocks) for blocks, _ in parts)
+
+
 def load(weight, parts, depth):
     return pl.pallas_call(
         functools.partial(load_kernel, parts, depth),
         out_shape=pltpu.VMEM(weight.shape, weight.dtype),
         in_specs=[HBM_SPEC],
         out_specs=pl.BlockSpec(memory_space=pltpu.VMEM),
-        scratch_shapes=[pltpu.SemaphoreType.DMA((SIDE * len(parts),))],
+        scratch_shapes=[pltpu.SemaphoreType.DMA((count_of(parts),))],
         cost_estimate=cost(1 << 31),
         compiler_params=pltpu.CompilerParams(vmem_limit_bytes=LIMIT),
     )(in_hbm(weight))
@@ -189,8 +226,8 @@
         in_specs=specs,
         out_specs=tuple(vmem_specs(2)),
         scratch_shapes=[
-            pltpu.VMEM((rows, depth_sum), jnp.bfloat16),
-            pltpu.SemaphoreType.DMA((SIDE * len(later),)),
+            pltpu.VMEM((rows, padded(depth_sum)), jnp.bfloat16),
+            pltpu.SemaphoreType.DMA((count_of(later),)),
         ],
         input_output_aliases=aliases,
         cost_estimate=cost(2 * rows * depth_sum * width),
@@ -210,7 +247,9 @@
         out_specs=pl.BlockSpec(memory_space=pltpu.VMEM),
         scratch_shapes=[
             pltpu.VMEM((rows, width), F32),
-            pltpu.VMEM((rows, depth_sum), jnp.bfloat16),
+            pltpu.VMEM((rows, LANES), F32),
+            pltpu.VMEM((rows, LANES), F32),
+            pltpu.VMEM((rows, padded(depth_sum)), jnp.bfloat16),
         ],
         cost_estimate=cost(2 * rows * depth_sum * width),
         compiler_params=pltpu.CompilerParams(vmem_limit_bytes=LIMIT),
@@ -261,10 +300,8 @@
     pack[...] = as_columns(sums, info[...])
 
 
-def loss_kernel(prompts, *refs):
-    packs, (advantage, loss) = refs[:-2], refs[-2:]
-    rolls = packs[0].shape[0]
-    every = jnp.concatenate([p[...] for p in packs], axis=0)
+def loss_kernel(prompts, rolls, pack, advantage, loss):
+    every = pack[...]
     low, high, extra, count, score, prompt = (every[:, k : k + 1] for k in range(6))
     gain = jnp.zeros_like(score)
     for g in range(prompts):
@@ -291,49 +328,57 @@
 
 def per_device(hidden, weight, targets, old_logprob, ref_logprob, lengths, rewards, group_ids):
     tok_rows, depth = hidden.shape
-    line = [hidden.T]
+    mine = hidden.T
+    line = [mine]
     for step in (1, -1, 2):
-        line.append(send_on(line[0], 0, step))
+        line.append(send_on(mine, 0, step))
+    sides = []
+    for step in (1, -1):
+        sides.append(send_on(mine, 1, step))
+    others = STEPS[1:]
     sets = (
-        ((0, 0), (0, 1)),
-        ((-1, 0), (1, 0)),
-        ((-1, 1), (1, 1)),
-        ((2, 0), (2, 1)),
+        ((LINE, 0), (LINE, 1)),
+        ((SIDES, 0), (SIDES, 1)),
+        ((far_blocks(2), 0),),
+        ((far_blocks(2), 1),),
+        ((far_blocks(-1, others), 0), (far_blocks(1, others), 0)),
+        ((far_blocks(-1, others), 1), (far_blocks(1, others), 1)),
     )
     held = load(weight, sets[0], depth)
     line = jnp.concatenate(line, axis=0)
+    far, far_p = {}, {}
+    for step in (2, 1, -1):
+        far[step] = send_on(line if step == 2 else line[depth:], 1, step)
     line_p = swap(line)
-    far, far_p = [], []
-    for step in (1, -1, 2):
-        far.append(send_on(line, 1, step))
+    sides = jnp.concatenate(sides, axis=0)
+    sides_p = swap(sides)
     acc, held = product((line, line_p), sets[0], sets[1], held, weight, None)
-    for k in range(3):
-        far_p.append(swap(far[k]))
-    acc, held = product(far[:2], sets[1], sets[2], held, weight, acc)
-    acc, held = product(far_p[:2], sets[2], sets[3], held, weight, acc)
+    acc, held = product((sides, sides_p), sets[1], sets[2], held, weight, acc)
+    for step in (2, 1, -1):
+        far_p[step] = swap(far[step])
+    acc, held = product((far[2],), sets[2], sets[3], held, weight, acc)
+    acc, held = product((far_p[2],), sets[3], sets[4], held, weight, acc)
+    acc, held = product((far[1], far[-1]), sets[4], sets[5], held, weight, acc)
     target = jnp.broadcast_to(targets[:, None], (tok_rows, LANES))
-    lines = statistics((far[2], far_p[2]), sets[3], held, acc, target)
+    lines = statistics((far_p[1], far_p[-1]), sets[5], held, acc, target)
     lines = lax.all_to_all(lines, "vocab", 0, 0, tiled=True)
     rolls = rewards.shape[0]
     own, position = own_rolls(rolls, tok_rows)
     live = (own & (position < lengths[:, None])).astype(F32)
     blank = jnp.zeros((rolls, 1), F32)
-    info = as_columns(
-        [blank] * 4 + [rewards.astype(F32)[:, None], group_ids.astype(F32)[:, None]]
-    )
+    info = as_columns([blank] * 4 + [rewards.astype(F32)[:, None], group_ids.astype(F32)[:, None]])
     row = (1, tok_rows)
     token_logprob, entropy, pack = small(
         token_kernel,
         (lines, old_logprob[None], ref_logprob[None], live, info),
         (row, row, (rolls, LANES)),
     )
-    size = lax.axis_size("dp")
-    packs = [
-        lax.ppermute(pack, "dp", [(v, (v + step) % size) for v in range(size)])
-        for step in range(1, size)
-    ]
+    for mask in (1, 3):
+        pairs = [(v, v ^ mask) for v in range(lax.axis_size("dp"))]
+        pack = jnp.concatenate([pack, lax.ppermute(pack, "dp", pairs)], axis=0)
+    prompts = rolls * lax.axis_size("dp") // GROUP
     advantage, loss = small(
-        functools.partial(loss_kernel, rolls * size // GROUP), (pack, *packs), (row, (1, 1))
+        functools.partial(loss_kernel, prompts, rolls), (pack,), (row, (1, 1))
     )
     return (token_logprob[0], entropy[0], advantage[0], loss[0, 0])
 

time: 75 us -> 78.2 us (1.043)
  Pallas kernels: 21.8 us -> 24 us
  waiting for transfers between devices: 23.3 us -> 24.6 us
    ppermute x6 -> x8, starting transfers between devices: 10.6 us -> 14 us  [send_on(): return lax.ppermute(value, 'vocab', pairs)]
    pallas_call x3 -> x5, Pallas kernels: 11.5 us -> 14.6 us  [product(): pl.pallas_call(functools.partial(step_kernel, parts, later, depth), out_s...]
    ppermute x4 -> x5, starting transfers between devices: 3.64 us -> 1.17 us  [swap(): return lax.ppermute(value, 'vocab', pairs)]
    all_to_all x1, starting transfers between devices: 5.43 us -> 4.58 us  [per_device(): lines = lax.all_to_all(lines, 'vocab', 0, 0, tiled=True)]
    pallas_call x1, Pallas kernels: 5.83 us -> 5.02 us  [statistics(): pl.pallas_call(functools.partial(last_kernel, parts, held.shape[0] // siz...]
    ppermute x3 -> x2, waiting for transfers between devices: 2.59 us -> 3.32 us  [per_device(): pack = jnp.concatenate([pack, lax.ppermute(pack, 'dp', pairs)], axis=0)]
    ppermute x3 -> x2, starting transfers between devices: 6.52 us -> 5.94 us  [per_device(): pack = jnp.concatenate([pack, lax.ppermute(pack, 'dp', pairs)], axis=0)]
    ppermute x6 -> x8, waiting for transfers between devices: 12.1 us -> 12.6 us  [send_on(): return lax.ppermute(value, 'vocab', pairs)]
  transfers between devices with their start and end apart: 14 -> 16, of which waited for: 9 -> 5; matrix products, arithmetic and copies ran while one was open for 2% -> 3% of each run, Pallas kernels for 19% -> 22%
where the time goes in v3:
time: 78.2 us; the launch traced here: 77.9 us
  starting transfers between devices  25.7 us (33%)
  waiting for transfers between devices  24.6 us (31%)
  Pallas kernels  24 us (31%)
  other arithmetic  2.45 us (3%)
  between operations  0.87 us (1%)
    pallas_call x5, Pallas kernels, product(): pl.pallas_call(functools.partial(step_kernel, parts, later, depth), out_s...  14.6 us
    ppermute x8, starting transfers between devices, send_on(): return lax.ppermute(value, 'vocab', pairs)  14 us
    ppermute x8, waiting for transfers between devices, send_on(): return lax.ppermute(value, 'vocab', pairs)  12.6 us
    all_to_all x1, waiting for transfers between devices, per_device(): lines = lax.all_to_all(lines, 'vocab', 0, 0, tiled=True)  8.68 us
    ppermute x2, starting transfers between devices, per_device(): pack = jnp.concatenate([pack, lax.ppermute(pack, 'dp', pairs)], axis=0)  5.94 us
    pallas_call x1, Pallas kernels, statistics(): pl.pallas_call(functools.partial(last_kernel, parts, held.shape[0] // siz...  5.02 us
    all_to_all x1, starting transfers between devices, per_device(): lines = lax.all_to_all(lines, 'vocab', 0, 0, tiled=True)  4.58 us
    ppermute x2, waiting for transfers between devices, per_device(): pack = jnp.concatenate([pack, lax.ppermute(pack, 'dp', pairs)], axis=0)  3.32 us
  transfers between devices with their start and end apart: 16, of which 5 were waited for; matrix products, arithmetic and copies ran while one was open for 3% of the time, Pallas kernels for 22%

profile of v3, /device:TPU:0, one launch (start us, length us, event | category | flops | bytes accessed | tf_op | source)
XLA Modules:
  0.0 77.9 jit_solution(9644397637253798235)
XLA Ops:
  0.6 1.7 %collective-permute-start = (bf16[160,512]{1,0:T(8,128)(2,1)}, bf16[160,512]{1,0:T(8,128)(2,1)S(1)}, u32[]{:S(2)}, u32[]{:S(2)}) collective-permute-start(bf16[160,512]{1,0:T(8,128)(2,1)} %bitcast.9), channel_id=1, source_target_pairs={{0,2},{1,9},{2,4},{3,11},{4,6},{5,13},{6,0},{7,15},{8,10},{9,17},{... | collective-permute-start | bytes 491528 | tf_op jit(solution)/shard_map/ppermute | solution.py:30
  2.3 1.6 %collective-permute-start.1 = (bf16[160,512]{1,0:T(8,128)(2,1)}, bf16[160,512]{1,0:T(8,128)(2,1)S(1)}, u32[]{:S(2)}, u32[]{:S(2)}) collective-permute-start(bf16[160,512]{1,0:T(8,128)(2,1)} %bitcast.10), channel_id=1, source_target_pairs={{0,6},{1,25},{2,0},{3,27},{4,2},{5,29},{6,4},{7,31},{8,14},{9,1},{... | collective-permute-start | bytes 491528 | tf_op jit(solution)/shard_map/ppermute | solution.py:30
  3.9 1.9 %collective-permute-start.2 = (bf16[160,512]{1,0:T(8,128)(2,1)}, bf16[160,512]{1,0:T(8,128)(2,1)S(1)}, u32[]{:S(2)}, u32[]{:S(2)}) collective-permute-start(bf16[160,512]{1,0:T(8,128)(2,1)} %bitcast.11), channel_id=1, source_target_pairs={{0,4},{1,17},{2,6},{3,19},{4,0},{5,21},{6,2},{7,23},{8,12},{9,25},... | collective-permute-start | bytes 491528 | tf_op jit(solution)/shard_map/ppermute | solution.py:30
  5.9 1.6 %collective-permute-start.9 = (bf16[160,512]{1,0:T(8,128)(2,1)}, bf16[160,512]{1,0:T(8,128)(2,1)S(1)}, u32[]{:S(2)}, u32[]{:S(2)}) collective-permute-start(bf16[160,512]{1,0:T(8,128)(2,1)} %bitcast.12), channel_id=1, source_target_pairs={{0,8},{1,3},{2,10},{3,5},{4,12},{5,7},{6,14},{7,1},{8,16},{9,11},{... | collective-permute-start | bytes 491528 | tf_op jit(solution)/shard_map/ppermute | solution.py:30
  7.4 0.7 convert_element_type.10
  8.1 0.7 convert_element_type.11
  8.8 0.1 select_select_fusion.info
  8.8 0.0 collective-permute-done
  8.8 0.0 collective-permute-done.1
  8.8 3.1 %collective-permute-done.2 = bf16[160,512]{1,0:T(8,128)(2,1)S(1)} collective-permute-done((bf16[160,512]{1,0:T(8,128)(2,1)}, bf16[160,512]{1,0:T(8,128)(2,1)S(1)}, u32[]{:S(2)}, u32[]{:S(2)}) %collective-permute-start.2) | collective-permute-done | bytes 163872 | tf_op jit(solution)/shard_map/ppermute | solution.py:30
  11.9 1.0 %pad_maximum_fusion.refs_0_ = bf16[640,512]{1,0:T(8,128)(2,1)S(1)} fusion(bf16[160,512]{1,0:T(8,128)(2,1)S(1)} %collective-permute-done.2, bf16[160,512]{1,0:T(8,128)(2,1)S(1)} %collective-permute-done.1, bf16[160,512]{1,0:T(8,128)(2,1)S(1)} %collective-permute-done, bf16[160,512]{1,0:T(8,128)(2,1)} %bitcast.13), kind=kLoop, calls=%fused_computation | loop fusion | flops 2621440 | bytes 1310720 | tf_op jit(solution)/shard_map/concatenate | solution.py:348
  12.9 0.1 collective-permute-start.12
  13.0 3.4 %collective-permute-start.7 = (bf16[640,512]{1,0:T(8,128)(2,1)S(1)}, bf16[640,512]{1,0:T(8,128)(2,1)S(1)}, u32[]{:S(2)}, u32[]{:S(2)}) collective-permute-start(bf16[640,512]{1,0:T(8,128)(2,1)S(1)} %pad_maximum_fusion.refs_0_), channel_id=1, source_target_pairs={{0,16},{1,5},{2,18},{3,7},{4,20},{5,1},{6,22},{7,3},{8,24},{9,13},... | collective-permute-start | bytes 1966088 | tf_op jit(solution)/shard_map/ppermute | solution.py:30
  16.4 0.0 copy-start.2
  16.4 0.7 collective-permute-start.3
  17.2 2.6 %collective-permute-start.5 = (bf16[480,512]{1,0:T(8,128)(2,1)S(1)}, bf16[480,512]{1,0:T(8,128)(2,1)S(1)}, u32[]{:S(2)}, u32[]{:S(2)}) collective-permute-start(bf16[480,512]{1,0:T(8,128)(2,1)S(1)} %constant_dynamic-update-slice_fusion), channel_id=1, source_target_pairs={{0,24},{1,7},{2,26},{3,1},{4,28},{5,3},{6,30},{7,5},{8,0},{9,15},{... | collective-permute-start | bytes 1474568 | tf_op jit(solution)/shard_map/ppermute | solution.py:30
  19.8 2.8 %shard_map.111.refs_2_ = bf16[5120,2432]{1,0:T(8,128)(2,1)S(1)} custom-call(bf16[5120,2432]{1,0:T(8,128)(2,1)} %refs_3_.5), custom_call_target="tpu_custom_call" | custom-call | flops 2147483648 | bytes 1048576 | tf_op jit(solution)/shard_map/pallas_call | solution.py:199
  22.6 0.0 collective-permute-done.9
  22.6 0.0 copy-done.2
  22.6 0.5 collective-permute-start.10
  23.1 9.5 %collective-permute-done.10 = bf16[160,512]{1,0:T(8,128)(2,1)S(1)} collective-permute-done((bf16[160,512]{1,0:T(8,128)(2,1)S(1)}, bf16[160,512]{1,0:T(8,128)(2,1)S(1)}, u32[]{:S(2)}, u32[]{:S(2)}) %collective-permute-start.10) | collective-permute-done | bytes 163872 | tf_op jit(solution)/shard_map/ppermute | solution.py:30
  32.7 0.1 collective-permute-start.11
  32.8 0.0 collective-permute-done.7.refs_0_
  32.8 0.5 collective-permute-start.8
  33.3 0.0 collective-permute-done.3.refs_0_
  33.3 0.1 collective-permute-start.4
  33.4 0.0 collective-permute-done.5.refs_1_
  33.4 0.4 collective-permute-start.6
  33.8 0.0 collective-permute-done.12.refs_1_
  33.8 3.7 %shard_map.112 = (f32[512,2432]{1,0:T(8,128)S(1)}, bf16[5120,2432]{1,0:T(8,128)(2,1)S(1)}) custom-call(bf16[640,512]{1,0:T(8,128)(2,1)S(1)} %pad_maximum_fusion.refs_0_, bf16[640,512]{1,0:T(8,128)(2,1)S(1)} %collective-permute-done.12.refs_1_, bf16[5120,2432]{1,0:T(8,128)(2,1)S(1)} %shard_map.111.refs_2_, ...), custom_call_target="tpu_custom_call", output_to_operand_aliasing={{1}: (2, {})} | custom-call | flops 3187671040 | bytes 1048576 | tf_op jit(solution)/shard_map/pallas_call | solution.py:220
  37.5 0.0 collective-permute-done.11.refs_1_
  37.5 2.6 %shard_map.113 = (f32[512,2432]{1,0:T(8,128)S(1)}, bf16[5120,2432]{1,0:T(8,128)(2,1)S(1)}) custom-call(bf16[320,512]{1,0:T(8,128)(2,1)S(1)} %constant_dynamic-update-slice_fusion.3.refs_0_, bf16[320,512]{1,0:T(8,128)(2,1)S(1)} %collective-permute-done.11.refs_1_, ...), custom_call_target="tpu_custom_call", output_to_operand_aliasing={{1}: (2, {}), {0}: (4, {})} | custom-call | flops 1593835520 | bytes 1048576 | tf_op jit(solution)/shard_map/pallas_call | solution.py:220
  40.1 2.6 %shard_map.114 = (f32[512,2432]{1,0:T(8,128)S(1)}, bf16[5120,2432]{1,0:T(8,128)(2,1)S(1)}) custom-call(bf16[640,512]{1,0:T(8,128)(2,1)S(1)} %collective-permute-done.7.refs_0_, bf16[5120,2432]{1,0:T(8,128)(2,1)S(1)} %get-tuple-element.21.refs_1_, bf16[5120,2432]{1,0:T(8,128)(2,1)} %refs_3_.5, ...), custom_call_target="tpu_custom_call", output_to_operand_aliasing={{1}: (1, {}), {0}: (3, {})} | custom-call | flops 1593835520 | bytes 1048576 | tf_op jit(solution)/shard_map/pallas_call | solution.py:220
  42.6 0.0 collective-permute-done.8.refs_0_
  42.6 2.6 %shard_map.115 = (f32[512,2432]{1,0:T(8,128)S(1)}, bf16[5120,2432]{1,0:T(8,128)(2,1)S(1)}) custom-call(bf16[640,512]{1,0:T(8,128)(2,1)S(1)} %collective-permute-done.8.refs_0_, bf16[5120,2432]{1,0:T(8,128)(2,1)S(1)} %get-tuple-element.23.refs_1_, bf16[5120,2432]{1,0:T(8,128)(2,1)} %refs_3_.5, ...), custom_call_target="tpu_custom_call", output_to_operand_aliasing={{1}: (1, {}), {0}: (3, {})} | custom-call | flops 1593835520 | bytes 1048576 | tf_op jit(solution)/shard_map/pallas_call | solution.py:220
  45.2 0.0 copy-start.3
  45.2 3.3 %shard_map.116 = (f32[512,2432]{1,0:T(8,128)S(1)}, bf16[5120,2432]{1,0:T(8,128)(2,1)S(1)}) custom-call(bf16[480,512]{1,0:T(8,128)(2,1)S(1)} %collective-permute-done.3.refs_0_, bf16[480,512]{1,0:T(8,128)(2,1)S(1)} %collective-permute-done.5.refs_1_, bf16[5120,2432]{1,0:T(8,128)(2,1)S(1)} %get-tuple-element.25.refs_2_, ...), custom_call_target="tpu_custom_call", output_to_operand_aliasing={{1}: (2, {}), {0}: (4, {})} | custom-call | flops 2390753280 | bytes 1048576 | tf_op jit(solution)/shard_map/pallas_call | solution.py:220
  48.5 0.0 collective-permute-done.4.refs_0_
  48.5 0.0 collective-permute-done.6.refs_1_
  48.5 0.0 copy-done.3
  48.5 0.1 broadcast_in_dim.41.refs_4_
  48.6 0.0 copy-start.4
  48.6 0.0 copy-start
  48.7 0.0 copy-start.1
  48.7 5.0 %shard_map.117 = f32[32,4,512]{2,1,0:T(4,128)} custom-call(bf16[480,512]{1,0:T(8,128)(2,1)S(1)} %collective-permute-done.4.refs_0_, bf16[480,512]{1,0:T(8,128)(2,1)S(1)} %collective-permute-done.6.refs_1_, bf16[5120,2432]{1,0:T(8,128)(2,1)S(1)} %get-tuple-element.27.refs_2_, f32[512,2432]{1,0:T(8,128)S(1)} %get-tuple-element.28.refs_3_, ...), custom_call_target="tpu_custom_call" | custom-call | flops 2390753280 | bytes 1048576 | tf_op jit(solution)/shard_map/pallas_call | solution.py:243
  53.7 4.6 %all-to-all-start = ((f32[32,4,512]{2,1,0:T(4,128)}), f32[32,4,512]{2,1,0:T(4,128)S(1)}, u32[]{:S(2)}, u32[]{:S(2)}) async-start(f32[32,4,512]{2,1,0:T(4,128)} %shard_map.117), calls=%async_computation | async-start | bytes 524288 | tf_op jit(solution)/shard_map/all_to_all | solution.py:364
  58.3 0.0 copy-done.4
  58.3 0.1 fusion.1.live
  58.4 8.7 %all-to-all-done.lines = f32[32,4,512]{2,1,0:T(4,128)S(1)} async-done(((f32[32,4,512]{2,1,0:T(4,128)}), f32[32,4,512]{2,1,0:T(4,128)S(1)}, u32[]{:S(2)}, u32[]{:S(2)}) %all-to-all-start) | async-done | bytes 262176 | tf_op jit(solution)/shard_map/all_to_all | solution.py:364
  67.1 0.0 copy-done
  67.1 0.0 copy-done.1
  67.1 0.7 shard_map.118
  67.7 1.9 %collective-permute-start.13 = (f32[8,128]{1,0:T(8,128)S(1)}, f32[8,128]{1,0:T(8,128)S(1)}, u32[]{:S(2)}, u32[]{:S(2)}) collective-permute-start(f32[8,128]{1,0:T(8,128)S(1)} %get-tuple-element.31), channel_id=1, source_target_pairs={{0,32},{32,0},{64,96},{96,64},{1,33},{33,1},{65,97},{97,65},{2,34}... | collective-permute-start | bytes 12296 | tf_op jit(solution)/shard_map/ppermute | solution.py:378
  69.7 1.7 %collective-permute-done.13 = f32[8,128]{1,0:T(8,128)S(1)} collective-permute-done((f32[8,128]{1,0:T(8,128)S(1)}, f32[8,128]{1,0:T(8,128)S(1)}, u32[]{:S(2)}, u32[]{:S(2)}) %collective-permute-start.13) | collective-permute-done | bytes 4128 | tf_op jit(solution)/shard_map/ppermute | solution.py:378
  71.3 4.0 %collective-permute-start.14 = (f32[16,128]{1,0:T(8,128)S(1)}, f32[16,128]{1,0:T(8,128)S(1)}, u32[]{:S(2)}, u32[]{:S(2)}) collective-permute-start(f32[16,128]{1,0:T(8,128)S(1)} %pad_maximum_fusion.2), channel_id=1, source_target_pairs={{0,96},{32,64},{64,32},{96,0},{1,97},{33,65},{65,33},{97,1},{2,98}... | collective-permute-start | bytes 24584 | tf_op jit(solution)/shard_map/ppermute | solution.py:378
  75.4 1.6 %collective-permute-done.14 = f32[16,128]{1,0:T(8,128)S(1)} collective-permute-done((f32[16,128]{1,0:T(8,128)S(1)}, f32[16,128]{1,0:T(8,128)S(1)}, u32[]{:S(2)}, u32[]{:S(2)}) %collective-permute-start.14) | collective-permute-done | bytes 8224 | tf_op jit(solution)/shard_map/ppermute | solution.py:378
  77.0 0.9 %shard_map.119 = (f32[1,512]{1,0:T(1,128)}, f32[1,1]{1,0:T(1,128)}) custom-call(f32[32,128]{1,0:T(8,128)S(1)} %pad_maximum_fusion.1.pack), custom_call_target="tpu_custom_call" | custom-call | tf_op jit(solution)/shard_map/pallas_call | solution.py:320
  (11 shorter events, 0.1 us)
Async XLA Ops:
  0.6 8.2 %collective-permute-start = (bf16[160,512]{1,0:T(8,128)(2,1)}, bf16[160,512]{1,0:T(8,128)(2,1)S(1)}, u32[]{:S(2)}, u32[]{:S(2)}) collective-permute-start(bf16[160,512]{1,0:T(8,128)(2,1)} %bitcast.9), channel_id=1, source_target_pairs={{0,2},{1,9},{2,4},{3,11},{4,6},{5,13},{6,0},{7,15},{8,10},{9,17},{... | collective-permute-start | bytes 491528 | tf_op jit(solution)/shard_map/ppermute | solution.py:30
  2.3 6.5 %collective-permute-start.1 = (bf16[160,512]{1,0:T(8,128)(2,1)}, bf16[160,512]{1,0:T(8,128)(2,1)S(1)}, u32[]{:S(2)}, u32[]{:S(2)}) collective-permute-start(bf16[160,512]{1,0:T(8,128)(2,1)} %bitcast.10), channel_id=1, source_target_pairs={{0,6},{1,25},{2,0},{3,27},{4,2},{5,29},{6,4},{7,31},{8,14},{9,1},{... | collective-permute-start | bytes 491528 | tf_op jit(solution)/shard_map/ppermute | solution.py:30
  3.9 8.0 %collective-permute-start.2 = (bf16[160,512]{1,0:T(8,128)(2,1)}, bf16[160,512]{1,0:T(8,128)(2,1)S(1)}, u32[]{:S(2)}, u32[]{:S(2)}) collective-permute-start(bf16[160,512]{1,0:T(8,128)(2,1)} %bitcast.11), channel_id=1, source_target_pairs={{0,4},{1,17},{2,6},{3,19},{4,0},{5,21},{6,2},{7,23},{8,12},{9,25},... | collective-permute-start | bytes 491528 | tf_op jit(solution)/shard_map/ppermute | solution.py:30
  5.9 16.7 %collective-permute-start.9 = (bf16[160,512]{1,0:T(8,128)(2,1)}, bf16[160,512]{1,0:T(8,128)(2,1)S(1)}, u32[]{:S(2)}, u32[]{:S(2)}) collective-permute-start(bf16[160,512]{1,0:T(8,128)(2,1)} %bitcast.12), channel_id=1, source_target_pairs={{0,8},{1,3},{2,10},{3,5},{4,12},{5,7},{6,14},{7,1},{8,16},{9,11},{... | collective-permute-start | bytes 491528 | tf_op jit(solution)/shard_map/ppermute | solution.py:30
  12.9 20.9 %collective-permute-start.12 = (bf16[640,512]{1,0:T(8,128)(2,1)S(1)}, bf16[640,512]{1,0:T(8,128)(2,1)S(1)}, u32[]{:S(2)}, u32[]{:S(2)}) collective-permute-start(bf16[640,512]{1,0:T(8,128)(2,1)S(1)} %pad_maximum_fusion.refs_0_), channel_id=1, source_target_pairs={{0,1},{1,0},{2,3},{3,2},{4,5},{5,4},{6,7},{7,6},{8,9},{9,8},{10,11... | collective-permute-start | bytes 1966088 | tf_op jit(solution)/shard_map/ppermute | solution.py:35
  13.0 19.8 %collective-permute-start.7 = (bf16[640,512]{1,0:T(8,128)(2,1)S(1)}, bf16[640,512]{1,0:T(8,128)(2,1)S(1)}, u32[]{:S(2)}, u32[]{:S(2)}) collective-permute-start(bf16[640,512]{1,0:T(8,128)(2,1)S(1)} %pad_maximum_fusion.refs_0_), channel_id=1, source_target_pairs={{0,16},{1,5},{2,18},{3,7},{4,20},{5,1},{6,22},{7,3},{8,24},{9,13},... | collective-permute-start | bytes 1966088 | tf_op jit(solution)/shard_map/ppermute | solution.py:30
  16.4 6.2 %copy-start.2 = (bf16[512,160]{0,1:T(8,128)(2,1)S(1)}, bf16[512,160]{0,1:T(8,128)(2,1)}, u32[]{:S(2)}) copy-start(bf16[512,160]{0,1:T(8,128)(2,1)} %param.8) | copy-start | bytes 491524
  16.4 16.9 %collective-permute-start.3 = (bf16[480,512]{1,0:T(8,128)(2,1)S(1)}, bf16[480,512]{1,0:T(8,128)(2,1)S(1)}, u32[]{:S(2)}, u32[]{:S(2)}) collective-permute-start(bf16[480,512]{1,0:T(8,128)(2,1)S(1)} %constant_dynamic-update-slice_fusion), channel_id=1, source_target_pairs={{0,8},{1,3},{2,10},{3,5},{4,12},{5,7},{6,14},{7,1},{8,16},{9,11},{... | collective-permute-start | bytes 1474568 | tf_op jit(solution)/shard_map/ppermute | solution.py:30
  17.2 16.2 %collective-permute-start.5 = (bf16[480,512]{1,0:T(8,128)(2,1)S(1)}, bf16[480,512]{1,0:T(8,128)(2,1)S(1)}, u32[]{:S(2)}, u32[]{:S(2)}) collective-permute-start(bf16[480,512]{1,0:T(8,128)(2,1)S(1)} %constant_dynamic-update-slice_fusion), channel_id=1, source_target_pairs={{0,24},{1,7},{2,26},{3,1},{4,28},{5,3},{6,30},{7,5},{8,0},{9,15},{... | collective-permute-start | bytes 1474568 | tf_op jit(solution)/shard_map/ppermute | solution.py:30
  22.6 10.1 %collective-permute-start.10 = (bf16[160,512]{1,0:T(8,128)(2,1)S(1)}, bf16[160,512]{1,0:T(8,128)(2,1)S(1)}, u32[]{:S(2)}, u32[]{:S(2)}) collective-permute-start(bf16[160,512]{1,0:T(8,128)(2,1)S(1)} %bitcast.14), channel_id=1, source_target_pairs={{0,24},{1,7},{2,26},{3,1},{4,28},{5,3},{6,30},{7,5},{8,0},{9,15},{... | collective-permute-start | bytes 491528 | tf_op jit(solution)/shard_map/ppermute | solution.py:30
  32.7 4.8 %collective-permute-start.11 = (bf16[320,512]{1,0:T(8,128)(2,1)S(1)}, bf16[320,512]{1,0:T(8,128)(2,1)S(1)}, u32[]{:S(2)}, u32[]{:S(2)}) collective-permute-start(bf16[320,512]{1,0:T(8,128)(2,1)S(1)} %constant_dynamic-update-slice_fusion.3.refs_0_), channel_id=1, source_target_pairs={{0,1},{1,0},{2,3},{3,2},{4,5},{5,4},{6,7},{7,6},{8,9},{9,8},{10,11... | collective-permute-start | bytes 983048 | tf_op jit(solution)/shard_map/ppermute | solution.py:35
  32.8 9.8 %collective-permute-start.8 = (bf16[640,512]{1,0:T(8,128)(2,1)S(1)}, bf16[640,512]{1,0:T(8,128)(2,1)S(1)}, u32[]{:S(2)}, u32[]{:S(2)}) collective-permute-start(bf16[640,512]{1,0:T(8,128)(2,1)S(1)} %collective-permute-done.7.refs_0_), channel_id=1, source_target_pairs={{0,1},{1,0},{2,3},{3,2},{4,5},{5,4},{6,7},{7,6},{8,9},{9,8},{10,11... | collective-permute-start | bytes 1966088 | tf_op jit(solution)/shard_map/ppermute | solution.py:35
  33.3 15.2 %collective-permute-start.4 = (bf16[480,512]{1,0:T(8,128)(2,1)S(1)}, bf16[480,512]{1,0:T(8,128)(2,1)S(1)}, u32[]{:S(2)}, u32[]{:S(2)}) collective-permute-start(bf16[480,512]{1,0:T(8,128)(2,1)S(1)} %collective-permute-done.3.refs_0_), channel_id=1, source_target_pairs={{0,1},{1,0},{2,3},{3,2},{4,5},{5,4},{6,7},{7,6},{8,9},{9,8},{10,11... | collective-permute-start | bytes 1474568 | tf_op jit(solution)/shard_map/ppermute | solution.py:35
  33.4 15.1 %collective-permute-start.6 = (bf16[480,512]{1,0:T(8,128)(2,1)S(1)}, bf16[480,512]{1,0:T(8,128)(2,1)S(1)}, u32[]{:S(2)}, u32[]{:S(2)}) collective-permute-start(bf16[480,512]{1,0:T(8,128)(2,1)S(1)} %collective-permute-done.5.refs_1_), channel_id=1, source_target_pairs={{0,1},{1,0},{2,3},{3,2},{4,5},{5,4},{6,7},{7,6},{8,9},{9,8},{10,11... | collective-permute-start | bytes 1474568 | tf_op jit(solution)/shard_map/ppermute | solution.py:35
  45.2 3.3 %copy-start.3 = (s32[512]{0:T(512)S(1)}, s32[512]{0:T(512)}, u32[]{:S(2)}) copy-start(s32[512]{0:T(512)} %param.10) | copy-start | bytes 6148
  48.6 9.7 %copy-start.4 = (s32[8]{0:T(128)S(1)}, s32[8]{0:T(128)}, u32[]{:S(2)}) copy-start(s32[8]{0:T(128)} %param.13) | copy-start | bytes 100
  48.6 18.4 %copy-start = (f32[512]{0:T(512)S(1)}, f32[512]{0:T(512)}, u32[]{:S(2)}) copy-start(f32[512]{0:T(512)} %param.11) | copy-start | bytes 6148
  48.7 18.4 %copy-start.1 = (f32[512]{0:T(512)S(1)}, f32[512]{0:T(512)}, u32[]{:S(2)}) copy-start(f32[512]{0:T(512)} %param.12) | copy-start | bytes 6148
  53.7 13.4 %all-to-all-start = ((f32[32,4,512]{2,1,0:T(4,128)}), f32[32,4,512]{2,1,0:T(4,128)S(1)}, u32[]{:S(2)}, u32[]{:S(2)}) async-start(f32[32,4,512]{2,1,0:T(4,128)} %shard_map.117), calls=%async_computation | async-start | bytes 524288 | tf_op jit(solution)/shard_map/all_to_all | solution.py:364
  67.7 3.6 %collective-permute-start.13 = (f32[8,128]{1,0:T(8,128)S(1)}, f32[8,128]{1,0:T(8,128)S(1)}, u32[]{:S(2)}, u32[]{:S(2)}) collective-permute-start(f32[8,128]{1,0:T(8,128)S(1)} %get-tuple-element.31), channel_id=1, source_target_pairs={{0,32},{32,0},{64,96},{96,64},{1,33},{33,1},{65,97},{97,65},{2,34}... | collective-permute-start | bytes 12296 | tf_op jit(solution)/shard_map/ppermute | solution.py:378
  71.3 5.7 %collective-permute-start.14 = (f32[16,128]{1,0:T(8,128)S(1)}, f32[16,128]{1,0:T(8,128)S(1)}, u32[]{:S(2)}, u32[]{:S(2)}) collective-permute-start(f32[16,128]{1,0:T(8,128)S(1)} %pad_maximum_fusion.2), channel_id=1, source_target_pairs={{0,96},{32,64},{64,32},{96,0},{1,97},{33,65},{65,33},{97,1},{2,98}... | collective-permute-start | bytes 24584 | tf_op jit(solution)/shard_map/ppermute | solution.py:378

commit v4 on v3

--- a/solution.py
+++ b/solution.py
@@ -123,50 +123,47 @@
 
 
 def last_kernel(parts, depth, *refs):
-    w_ref, acc_in, target, stats, acc, tops, picks, lhs = refs[len(parts) :]
-    tok, width = acc.shape
+    w_ref, acc_in, target, stats, tops, totals, moments, picks, lhs = refs[len(parts) :]
+    tok = acc_in.shape[0]
     step = 64
-    first = lax.axis_index("vocab") * width
-    lane = lax.broadcasted_iota(jnp.int32, (tok, LANES), 1) + first
+    first = lax.axis_index("vocab") * w_ref.shape[1]
+    lane = lax.broadcasted_iota(jnp.int32, (step, LANES), 1) + first
 
     def emit(b, e, out):
-        new = acc_in[:, b:e] + out
-        acc[:, b:e] = new
-        pieces = [new[:, k : k + LANES] for k in range(0, e - b, LANES)]
-        top = functools.reduce(jnp.maximum, pieces)
-        want = target[...] - lane
-        pick = jnp.zeros_like(top) if b == 0 else picks[...]
-        for k, piece in enumerate(pieces):
-            pick = jnp.where(want == b + k * LANES, piece, pick)
-        tops[...] = top if b == 0 else jnp.maximum(tops[...], top)
-        picks[...] = pick
+        for r in range(0, tok, step):
+            at = slice(r, r + step)
+            pieces = [
+                acc_in[at, k : k + LANES] + out[at, k - b : k - b + LANES]
+                for k in range(b, e, LANES)
+            ]
+            top = functools.reduce(jnp.maximum, pieces)
+            if b == 0:
+                total = moment = pick = jnp.zeros_like(top)
+            else:
+                before = tops[at, :]
+                top = jnp.maximum(before, top)
+                scale = jnp.exp(before - top)
+                total, moment = totals[at, :] * scale, moments[at, :] * scale
+                pick = picks[at, :]
+            want = target[at, :] - lane
+            for k, piece in enumerate(pieces):
+                scaled = jnp.exp(piece - top)
+                total += scaled
+                moment += scaled * piece
+                pick = jnp.where(want == b + k * LANES, piece, pick)
+            tops[at, :] = top
+            totals[at, :] = total
+            moments[at, :] = moment
+            picks[at, :] = pick
 
     multiply(refs[: len(parts)], parts, depth, w_ref, lhs, emit)
-    totals, moments = [], []
-    for r in range(0, tok, step):
-        top = tops[r : r + step, :]
-        total = jnp.zeros_like(top)
-        moment = jnp.zeros_like(top)
-        for b in range(0, width, LANES):
-            piece = acc[r : r + step, b : b + LANES]
-            scaled = jnp.exp(piece - top)
-            total += scaled
-            moment += scaled * piece
-        totals.append(total)
-        moments.append(moment)
-    total, moment = (jnp.concatenate(p, axis=0).T for p in (totals, moments))
-    top, pick = tops[...].T, picks[...].T
+    top, total, moment, pick = (ref[...].T for ref in (tops, totals, moments, picks))
     best = jnp.max(top, axis=0, keepdims=True)
     scale = jnp.exp(top - best)
-    mine = jnp.concatenate(
-        [
-            best,
-            jnp.sum(total * scale, axis=0, keepdims=True),
-            jnp.sum(moment * scale, axis=0, keepdims=True),
-            jnp.sum(pick, axis=0, keepdims=True),
-        ],
-        axis=0,
-    )
+    total = jnp.sum(total * scale, axis=0, keepdims=True)
+    moment = jnp.sum(moment * scale, axis=0, keepdims=True)
+    pick = jnp.sum(pick, axis=0, keepdims=True)
+    mine = jnp.concatenate([best + jnp.log(total), moment / total, pick], axis=1)
     for k in range(stats.shape[0]):
         stats[k] = mine
 
@@ -242,13 +239,11 @@
     operands = (*blocks, held, acc, target)
     return pl.pallas_call(
         functools.partial(last_kernel, parts, held.shape[0] // size),
-        out_shape=jax.ShapeDtypeStruct((size, 4, rows), F32),
+        out_shape=jax.ShapeDtypeStruct((size, 1, 3 * rows), F32),
         in_specs=vmem_specs(len(operands)),
         out_specs=pl.BlockSpec(memory_space=pltpu.VMEM),
         scratch_shapes=[
-            pltpu.VMEM((rows, width), F32),
-            pltpu.VMEM((rows, LANES), F32),
-            pltpu.VMEM((rows, LANES), F32),
+            *[pltpu.VMEM((rows, LANES), F32)] * 4,
             pltpu.VMEM((rows, padded(depth_sum)), jnp.bfloat16),
         ],
         cost_estimate=cost(2 * rows * depth_sum * width),
@@ -271,16 +266,20 @@
 
 
 def token_kernel(lines, old, ref, live, info, token_logprob, entropy, pack):
-    count = lines.shape[0]
-    top = lines[0, 0:1, :]
+    count, tok = lines.shape[0], old.shape[1]
+
+    def line(k, what):
+        return lines[k, 0:1, what * tok : (what + 1) * tok]
+
+    top = line(0, 0)
     for k in range(1, count):
-        top = jnp.maximum(top, lines[k, 0:1, :])
+        top = jnp.maximum(top, line(k, 0))
     total, moment, pick = (jnp.zeros_like(top) for _ in range(3))
     for k in range(count):
-        scale = jnp.exp(lines[k, 0:1, :] - top)
-        total += lines[k, 1:2, :] * scale
-        moment += lines[k, 2:3, :] * scale
-        pick += lines[k, 3:4, :]
+        scale = jnp.exp(line(k, 0) - top)
+        total += scale
+        moment += line(k, 1) * scale
+        pick += line(k, 2)
     lse = top + jnp.log(total)
     logprob = pick - lse
     spread = lse - moment / total

time: 78.2 us -> 75.5 us (0.965)
  waiting for transfers between devices: 24.6 us -> 21.6 us
  starting transfers between devices: 25.7 us -> 27.2 us
    ppermute x8, waiting for transfers between devices: 12.6 us -> 10.2 us  [send_on(): return lax.ppermute(value, 'vocab', pairs)]
    all_to_all x1, starting transfers between devices: 4.58 us -> 5.86 us  [per_device(): lines = lax.all_to_all(lines, 'vocab', 0, 0, tiled=True)]
    ppermute x8, starting transfers between devices: 14 us -> 15.2 us  [send_on(): return lax.ppermute(value, 'vocab', pairs)]
    ppermute x5, starting transfers between devices: 1.17 us -> 0.18 us  [swap(): return lax.ppermute(value, 'vocab', pairs)]
  transfers between devices with their start and end apart: 16 -> 16, of which waited for: 5 -> 7; matrix products, arithmetic and copies ran while one was open for 3% -> 2% of each run, Pallas kernels for 22% -> 23%
where the time goes in v4:
time: 75.5 us; the launch traced here: 75.3 us
  starting transfers between devices  27.2 us (36%)
  Pallas kernels  23.6 us (31%)
  waiting for transfers between devices  21.6 us (29%)
  other arithmetic  1.79 us (2%)
  between operations  0.88 us (1%)
    ppermute x8, starting transfers between devices, send_on(): return lax.ppermute(value, 'vocab', pairs)  15.2 us
    pallas_call x5, Pallas kernels, product(): pl.pallas_call(functools.partial(step_kernel, parts, later, depth), out_s...  14.6 us
    ppermute x8, waiting for transfers between devices, send_on(): return lax.ppermute(value, 'vocab', pairs)  10.2 us
    all_to_all x1, waiting for transfers between devices, per_device(): lines = lax.all_to_all(lines, 'vocab', 0, 0, tiled=True)  8.09 us
    ppermute x2, starting transfers between devices, per_device(): pack = jnp.concatenate([pack, lax.ppermute(pack, 'dp', pairs)], axis=0)  5.96 us
    all_to_all x1, starting transfers between devices, per_device(): lines = lax.all_to_all(lines, 'vocab', 0, 0, tiled=True)  5.86 us
    pallas_call x1, Pallas kernels, statistics(): pl.pallas_call(functools.partial(last_kernel, parts, held.shape[0] // siz...  4.6 us
    ppermute x2, waiting for transfers between devices, per_device(): pack = jnp.concatenate([pack, lax.ppermute(pack, 'dp', pairs)], axis=0)  3.32 us
  transfers between devices with their start and end apart: 16, of which 7 were waited for; matrix products, arithmetic and copies ran while one was open for 2% of the time, Pallas kernels for 23%

profile of v4, /device:TPU:0, one launch (start us, length us, event | category | flops | bytes accessed | tf_op | source)
XLA Modules:
  0.0 75.3 jit_solution(13676135356406073986)
XLA Ops:
  0.6 1.7 %collective-permute-start = (bf16[160,512]{1,0:T(8,128)(2,1)}, bf16[160,512]{1,0:T(8,128)(2,1)S(1)}, u32[]{:S(2)}, u32[]{:S(2)}) collective-permute-start(bf16[160,512]{1,0:T(8,128)(2,1)} %bitcast.9), channel_id=1, source_target_pairs={{0,2},{1,9},{2,4},{3,11},{4,6},{5,13},{6,0},{7,15},{8,10},{9,17},{... | collective-permute-start | bytes 491528 | tf_op jit(solution)/shard_map/ppermute | solution.py:30
  2.3 1.6 %collective-permute-start.1 = (bf16[160,512]{1,0:T(8,128)(2,1)}, bf16[160,512]{1,0:T(8,128)(2,1)S(1)}, u32[]{:S(2)}, u32[]{:S(2)}) collective-permute-start(bf16[160,512]{1,0:T(8,128)(2,1)} %bitcast.10), channel_id=1, source_target_pairs={{0,6},{1,25},{2,0},{3,27},{4,2},{5,29},{6,4},{7,31},{8,14},{9,1},{... | collective-permute-start | bytes 491528 | tf_op jit(solution)/shard_map/ppermute | solution.py:30
  3.9 1.9 %collective-permute-start.2 = (bf16[160,512]{1,0:T(8,128)(2,1)}, bf16[160,512]{1,0:T(8,128)(2,1)S(1)}, u32[]{:S(2)}, u32[]{:S(2)}) collective-permute-start(bf16[160,512]{1,0:T(8,128)(2,1)} %bitcast.11), channel_id=1, source_target_pairs={{0,4},{1,17},{2,6},{3,19},{4,0},{5,21},{6,2},{7,23},{8,12},{9,25},... | collective-permute-start | bytes 491528 | tf_op jit(solution)/shard_map/ppermute | solution.py:30
  5.9 1.6 %collective-permute-start.9 = (bf16[160,512]{1,0:T(8,128)(2,1)}, bf16[160,512]{1,0:T(8,128)(2,1)S(1)}, u32[]{:S(2)}, u32[]{:S(2)}) collective-permute-start(bf16[160,512]{1,0:T(8,128)(2,1)} %bitcast.12), channel_id=1, source_target_pairs={{0,8},{1,3},{2,10},{3,5},{4,12},{5,7},{6,14},{7,1},{8,16},{9,11},{... | collective-permute-start | bytes 491528 | tf_op jit(solution)/shard_map/ppermute | solution.py:30
  7.4 1.7 %collective-permute-start.10 = (bf16[160,512]{1,0:T(8,128)(2,1)}, bf16[160,512]{1,0:T(8,128)(2,1)S(1)}, u32[]{:S(2)}, u32[]{:S(2)}) collective-permute-start(bf16[160,512]{1,0:T(8,128)(2,1)} %bitcast.13), channel_id=1, source_target_pairs={{0,24},{1,7},{2,26},{3,1},{4,28},{5,3},{6,30},{7,5},{8,0},{9,15},{... | collective-permute-start | bytes 491528 | tf_op jit(solution)/shard_map/ppermute | solution.py:30
  9.1 0.7 fusion.1.live
  9.8 0.0 collective-permute-done
  9.8 0.0 collective-permute-done.1
  9.9 2.1 %collective-permute-done.2 = bf16[160,512]{1,0:T(8,128)(2,1)S(1)} collective-permute-done((bf16[160,512]{1,0:T(8,128)(2,1)}, bf16[160,512]{1,0:T(8,128)(2,1)S(1)}, u32[]{:S(2)}, u32[]{:S(2)}) %collective-permute-start.2) | collective-permute-done | bytes 163872 | tf_op jit(solution)/shard_map/ppermute | solution.py:30
  11.9 1.0 %pad_maximum_fusion.refs_0_ = bf16[640,512]{1,0:T(8,128)(2,1)S(1)} fusion(bf16[160,512]{1,0:T(8,128)(2,1)S(1)} %collective-permute-done.2, bf16[160,512]{1,0:T(8,128)(2,1)S(1)} %collective-permute-done.1, bf16[160,512]{1,0:T(8,128)(2,1)S(1)} %collective-permute-done, bf16[160,512]{1,0:T(8,128)(2,1)} %bitcast.14), kind=kLoop, calls=%fused_computation | loop fusion | flops 2621440 | bytes 1310720 | tf_op jit(solution)/shard_map/concatenate | solution.py:347
  12.9 0.1 collective-permute-start.12
  13.0 3.4 %collective-permute-start.7 = (bf16[640,512]{1,0:T(8,128)(2,1)S(1)}, bf16[640,512]{1,0:T(8,128)(2,1)S(1)}, u32[]{:S(2)}, u32[]{:S(2)}) collective-permute-start(bf16[640,512]{1,0:T(8,128)(2,1)S(1)} %pad_maximum_fusion.refs_0_), channel_id=1, source_target_pairs={{0,16},{1,5},{2,18},{3,7},{4,20},{5,1},{6,22},{7,3},{8,24},{9,13},... | collective-permute-start | bytes 1966088 | tf_op jit(solution)/shard_map/ppermute | solution.py:30
  16.4 0.0 copy-start.3
  16.4 0.0 copy-start.4
  16.5 0.7 collective-permute-start.3
  17.2 0.0 collective-permute-done.9
  17.2 2.6 %collective-permute-start.5 = (bf16[480,512]{1,0:T(8,128)(2,1)S(1)}, bf16[480,512]{1,0:T(8,128)(2,1)S(1)}, u32[]{:S(2)}, u32[]{:S(2)}) collective-permute-start(bf16[480,512]{1,0:T(8,128)(2,1)S(1)} %constant_dynamic-update-slice_fusion), channel_id=1, source_target_pairs={{0,24},{1,7},{2,26},{3,1},{4,28},{5,3},{6,30},{7,5},{8,0},{9,15},{... | collective-permute-start | bytes 1474568 | tf_op jit(solution)/shard_map/ppermute | solution.py:30
  19.8 2.8 %shard_map.111.refs_2_ = bf16[5120,2432]{1,0:T(8,128)(2,1)S(1)} custom-call(bf16[5120,2432]{1,0:T(8,128)(2,1)} %refs_3_.5), custom_call_target="tpu_custom_call" | custom-call | flops 2147483648 | bytes 1048576 | tf_op jit(solution)/shard_map/pallas_call | solution.py:196
  22.6 0.0 collective-permute-done.10
  22.7 0.1 collective-permute-start.11
  22.8 2.5 %collective-permute-done.7.refs_0_ = bf16[640,512]{1,0:T(8,128)(2,1)S(1)} collective-permute-done((bf16[640,512]{1,0:T(8,128)(2,1)S(1)}, bf16[640,512]{1,0:T(8,128)(2,1)S(1)}, u32[]{:S(2)}, u32[]{:S(2)}) %collective-permute-start.7) | collective-permute-done | bytes 655392 | tf_op jit(solution)/shard_map/ppermute | solution.py:30
  25.2 0.0 collective-permute-start.8
  25.2 0.0 copy-done.3
  25.3 0.0 copy-done.4
  25.3 5.1 %collective-permute-done.3.refs_0_ = bf16[480,512]{1,0:T(8,128)(2,1)S(1)} collective-permute-done((bf16[480,512]{1,0:T(8,128)(2,1)S(1)}, bf16[480,512]{1,0:T(8,128)(2,1)S(1)}, u32[]{:S(2)}, u32[]{:S(2)}) %collective-permute-start.3) | collective-permute-done | bytes 491552 | tf_op jit(solution)/shard_map/ppermute | solution.py:30
  30.4 0.0 collective-permute-start.4
  30.4 0.5 collective-permute-done.5.refs_1_
  30.9 0.0 collective-permute-start.6
  30.9 0.0 collective-permute-done.12.refs_1_
  30.9 3.7 %shard_map.112 = (f32[512,2432]{1,0:T(8,128)S(1)}, bf16[5120,2432]{1,0:T(8,128)(2,1)S(1)}) custom-call(bf16[640,512]{1,0:T(8,128)(2,1)S(1)} %pad_maximum_fusion.refs_0_, bf16[640,512]{1,0:T(8,128)(2,1)S(1)} %collective-permute-done.12.refs_1_, bf16[5120,2432]{1,0:T(8,128)(2,1)S(1)} %shard_map.111.refs_2_, ...), custom_call_target="tpu_custom_call", output_to_operand_aliasing={{1}: (2, {})} | custom-call | flops 3187671040 | bytes 1048576 | tf_op jit(solution)/shard_map/pallas_call | solution.py:217
  34.6 0.0 collective-permute-done.11.refs_1_
  34.6 2.5 %shard_map.113 = (f32[512,2432]{1,0:T(8,128)S(1)}, bf16[5120,2432]{1,0:T(8,128)(2,1)S(1)}) custom-call(bf16[320,512]{1,0:T(8,128)(2,1)S(1)} %constant_dynamic-update-slice_fusion.3.refs_0_, bf16[320,512]{1,0:T(8,128)(2,1)S(1)} %collective-permute-done.11.refs_1_, ...), custom_call_target="tpu_custom_call", output_to_operand_aliasing={{1}: (2, {}), {0}: (4, {})} | custom-call | flops 1593835520 | bytes 1048576 | tf_op jit(solution)/shard_map/pallas_call | solution.py:217
  37.2 2.6 %shard_map.114 = (f32[512,2432]{1,0:T(8,128)S(1)}, bf16[5120,2432]{1,0:T(8,128)(2,1)S(1)}) custom-call(bf16[640,512]{1,0:T(8,128)(2,1)S(1)} %collective-permute-done.7.refs_0_, bf16[5120,2432]{1,0:T(8,128)(2,1)S(1)} %get-tuple-element.21.refs_1_, bf16[5120,2432]{1,0:T(8,128)(2,1)} %refs_3_.5, ...), custom_call_target="tpu_custom_call", output_to_operand_aliasing={{1}: (1, {}), {0}: (3, {})} | custom-call | flops 1593835520 | bytes 1048576 | tf_op jit(solution)/shard_map/pallas_call | solution.py:217
  39.7 0.0 collective-permute-done.8.refs_0_
  39.7 2.6 %shard_map.115 = (f32[512,2432]{1,0:T(8,128)S(1)}, bf16[5120,2432]{1,0:T(8,128)(2,1)S(1)}) custom-call(bf16[640,512]{1,0:T(8,128)(2,1)S(1)} %collective-permute-done.8.refs_0_, bf16[5120,2432]{1,0:T(8,128)(2,1)S(1)} %get-tuple-element.23.refs_1_, bf16[5120,2432]{1,0:T(8,128)(2,1)} %refs_3_.5, ...), custom_call_target="tpu_custom_call", output_to_operand_aliasing={{1}: (1, {}), {0}: (3, {})} | custom-call | flops 1593835520 | bytes 1048576 | tf_op jit(solution)/shard_map/pallas_call | solution.py:217
  42.3 0.0 copy-start.2
  42.3 3.3 %shard_map.116 = (f32[512,2432]{1,0:T(8,128)S(1)}, bf16[5120,2432]{1,0:T(8,128)(2,1)S(1)}) custom-call(bf16[480,512]{1,0:T(8,128)(2,1)S(1)} %collective-permute-done.3.refs_0_, bf16[480,512]{1,0:T(8,128)(2,1)S(1)} %collective-permute-done.5.refs_1_, bf16[5120,2432]{1,0:T(8,128)(2,1)S(1)} %get-tuple-element.25.refs_2_, ...), custom_call_target="tpu_custom_call", output_to_operand_aliasing={{1}: (2, {}), {0}: (4, {})} | custom-call | flops 2390753280 | bytes 1048576 | tf_op jit(solution)/shard_map/pallas_call | solution.py:217
  45.6 0.0 collective-permute-done.4.refs_0_
  45.6 0.0 collective-permute-done.6.refs_1_
  45.6 0.0 copy-done.2
  45.6 0.1 broadcast_in_dim.41.refs_4_
  45.7 0.0 copy-start
  45.8 0.0 copy-start.1
  45.8 4.6 %shard_map.117 = f32[32,1,1536]{2,1,0:T(1,128)} custom-call(bf16[480,512]{1,0:T(8,128)(2,1)S(1)} %collective-permute-done.4.refs_0_, bf16[480,512]{1,0:T(8,128)(2,1)S(1)} %collective-permute-done.6.refs_1_, bf16[5120,2432]{1,0:T(8,128)(2,1)S(1)} %get-tuple-element.27.refs_2_, f32[512,2432]{1,0:T(8,128)S(1)} %get-tuple-element.28.refs_3_, ...), custom_call_target="tpu_custom_call" | custom-call | flops 2390753280 | bytes 1048576 | tf_op jit(solution)/shard_map/pallas_call | solution.py:240
  50.4 5.9 %all-to-all-start = ((f32[32,1,1536]{2,1,0:T(1,128)}), f32[32,1,1536]{2,1,0:T(1,128)S(1)}, u32[]{:S(2)}, u32[]{:S(2)}) async-start(f32[32,1,1536]{2,1,0:T(1,128)} %shard_map.117), calls=%async_computation | async-start | bytes 393216 | tf_op jit(solution)/shard_map/all_to_all | solution.py:363
  56.2 0.1 select_select_fusion.info
  56.3 8.1 %all-to-all-done.lines = f32[32,1,1536]{2,1,0:T(1,128)S(1)} async-done(((f32[32,1,1536]{2,1,0:T(1,128)}), f32[32,1,1536]{2,1,0:T(1,128)S(1)}, u32[]{:S(2)}, u32[]{:S(2)}) %all-to-all-start) | async-done | bytes 196640 | tf_op jit(solution)/shard_map/all_to_all | solution.py:363
  64.4 0.0 copy-done
  64.4 0.0 copy-done.1
  64.4 0.7 shard_map.118
  65.1 1.9 %collective-permute-start.13 = (f32[8,128]{1,0:T(8,128)S(1)}, f32[8,128]{1,0:T(8,128)S(1)}, u32[]{:S(2)}, u32[]{:S(2)}) collective-permute-start(f32[8,128]{1,0:T(8,128)S(1)} %get-tuple-element.31), channel_id=1, source_target_pairs={{0,32},{32,0},{64,96},{96,64},{1,33},{33,1},{65,97},{97,65},{2,34}... | collective-permute-start | bytes 12296 | tf_op jit(solution)/shard_map/ppermute | solution.py:377
  67.0 1.7 %collective-permute-done.13 = f32[8,128]{1,0:T(8,128)S(1)} collective-permute-done((f32[8,128]{1,0:T(8,128)S(1)}, f32[8,128]{1,0:T(8,128)S(1)}, u32[]{:S(2)}, u32[]{:S(2)}) %collective-permute-start.13) | collective-permute-done | bytes 4128 | tf_op jit(solution)/shard_map/ppermute | solution.py:377
  68.7 4.0 %collective-permute-start.14 = (f32[16,128]{1,0:T(8,128)S(1)}, f32[16,128]{1,0:T(8,128)S(1)}, u32[]{:S(2)}, u32[]{:S(2)}) collective-permute-start(f32[16,128]{1,0:T(8,128)S(1)} %pad_maximum_fusion.2), channel_id=1, source_target_pairs={{0,96},{32,64},{64,32},{96,0},{1,97},{33,65},{65,33},{97,1},{2,98}... | collective-permute-start | bytes 24584 | tf_op jit(solution)/shard_map/ppermute | solution.py:377
  72.7 1.6 %collective-permute-done.14 = f32[16,128]{1,0:T(8,128)S(1)} collective-permute-done((f32[16,128]{1,0:T(8,128)S(1)}, f32[16,128]{1,0:T(8,128)S(1)}, u32[]{:S(2)}, u32[]{:S(2)}) %collective-permute-start.14) | collective-permute-done | bytes 8224 | tf_op jit(solution)/shard_map/ppermute | solution.py:377
  74.4 0.9 %shard_map.119 = (f32[1,512]{1,0:T(1,128)}, f32[1,1]{1,0:T(1,128)}) custom-call(f32[32,128]{1,0:T(8,128)S(1)} %pad_maximum_fusion.1.pack), custom_call_target="tpu_custom_call" | custom-call | tf_op jit(solution)/shard_map/pallas_call | solution.py:319
  (13 shorter events, 0.1 us)
Async XLA Ops:
  0.6 9.2 %collective-permute-start = (bf16[160,512]{1,0:T(8,128)(2,1)}, bf16[160,512]{1,0:T(8,128)(2,1)S(1)}, u32[]{:S(2)}, u32[]{:S(2)}) collective-permute-start(bf16[160,512]{1,0:T(8,128)(2,1)} %bitcast.9), channel_id=1, source_target_pairs={{0,2},{1,9},{2,4},{3,11},{4,6},{5,13},{6,0},{7,15},{8,10},{9,17},{... | collective-permute-start | bytes 491528 | tf_op jit(solution)/shard_map/ppermute | solution.py:30
  2.3 7.5 %collective-permute-start.1 = (bf16[160,512]{1,0:T(8,128)(2,1)}, bf16[160,512]{1,0:T(8,128)(2,1)S(1)}, u32[]{:S(2)}, u32[]{:S(2)}) collective-permute-start(bf16[160,512]{1,0:T(8,128)(2,1)} %bitcast.10), channel_id=1, source_target_pairs={{0,6},{1,25},{2,0},{3,27},{4,2},{5,29},{6,4},{7,31},{8,14},{9,1},{... | collective-permute-start | bytes 491528 | tf_op jit(solution)/shard_map/ppermute | solution.py:30
  3.9 8.0 %collective-permute-start.2 = (bf16[160,512]{1,0:T(8,128)(2,1)}, bf16[160,512]{1,0:T(8,128)(2,1)S(1)}, u32[]{:S(2)}, u32[]{:S(2)}) collective-permute-start(bf16[160,512]{1,0:T(8,128)(2,1)} %bitcast.11), channel_id=1, source_target_pairs={{0,4},{1,17},{2,6},{3,19},{4,0},{5,21},{6,2},{7,23},{8,12},{9,25},... | collective-permute-start | bytes 491528 | tf_op jit(solution)/shard_map/ppermute | solution.py:30
  5.9 11.3 %collective-permute-start.9 = (bf16[160,512]{1,0:T(8,128)(2,1)}, bf16[160,512]{1,0:T(8,128)(2,1)S(1)}, u32[]{:S(2)}, u32[]{:S(2)}) collective-permute-start(bf16[160,512]{1,0:T(8,128)(2,1)} %bitcast.12), channel_id=1, source_target_pairs={{0,8},{1,3},{2,10},{3,5},{4,12},{5,7},{6,14},{7,1},{8,16},{9,11},{... | collective-permute-start | bytes 491528 | tf_op jit(solution)/shard_map/ppermute | solution.py:30
  7.4 15.2 %collective-permute-start.10 = (bf16[160,512]{1,0:T(8,128)(2,1)}, bf16[160,512]{1,0:T(8,128)(2,1)S(1)}, u32[]{:S(2)}, u32[]{:S(2)}) collective-permute-start(bf16[160,512]{1,0:T(8,128)(2,1)} %bitcast.13), channel_id=1, source_target_pairs={{0,24},{1,7},{2,26},{3,1},{4,28},{5,3},{6,30},{7,5},{8,0},{9,15},{... | collective-permute-start | bytes 491528 | tf_op jit(solution)/shard_map/ppermute | solution.py:30
  12.9 18.1 %collective-permute-start.12 = (bf16[640,512]{1,0:T(8,128)(2,1)S(1)}, bf16[640,512]{1,0:T(8,128)(2,1)S(1)}, u32[]{:S(2)}, u32[]{:S(2)}) collective-permute-start(bf16[640,512]{1,0:T(8,128)(2,1)S(1)} %pad_maximum_fusion.refs_0_), channel_id=1, source_target_pairs={{0,1},{1,0},{2,3},{3,2},{4,5},{5,4},{6,7},{7,6},{8,9},{9,8},{10,11... | collective-permute-start | bytes 1966088 | tf_op jit(solution)/shard_map/ppermute | solution.py:35
  13.0 12.3 %collective-permute-start.7 = (bf16[640,512]{1,0:T(8,128)(2,1)S(1)}, bf16[640,512]{1,0:T(8,128)(2,1)S(1)}, u32[]{:S(2)}, u32[]{:S(2)}) collective-permute-start(bf16[640,512]{1,0:T(8,128)(2,1)S(1)} %pad_maximum_fusion.refs_0_), channel_id=1, source_target_pairs={{0,16},{1,5},{2,18},{3,7},{4,20},{5,1},{6,22},{7,3},{8,24},{9,13},... | collective-permute-start | bytes 1966088 | tf_op jit(solution)/shard_map/ppermute | solution.py:30
  16.4 8.8 %copy-start.3 = (s32[8]{0:T(128)S(1)}, s32[8]{0:T(128)}, u32[]{:S(2)}) copy-start(s32[8]{0:T(128)} %param.15) | copy-start | bytes 100
  16.4 8.8 %copy-start.4 = (s32[8]{0:T(128)S(1)}, s32[8]{0:T(128)}, u32[]{:S(2)}) copy-start(s32[8]{0:T(128)} %param.14) | copy-start | bytes 100
  16.5 13.9 %collective-permute-start.3 = (bf16[480,512]{1,0:T(8,128)(2,1)S(1)}, bf16[480,512]{1,0:T(8,128)(2,1)S(1)}, u32[]{:S(2)}, u32[]{:S(2)}) collective-permute-start(bf16[480,512]{1,0:T(8,128)(2,1)S(1)} %constant_dynamic-update-slice_fusion), channel_id=1, source_target_pairs={{0,8},{1,3},{2,10},{3,5},{4,12},{5,7},{6,14},{7,1},{8,16},{9,11},{... | collective-permute-start | bytes 1474568 | tf_op jit(solution)/shard_map/ppermute | solution.py:30
  17.2 13.7 %collective-permute-start.5 = (bf16[480,512]{1,0:T(8,128)(2,1)S(1)}, bf16[480,512]{1,0:T(8,128)(2,1)S(1)}, u32[]{:S(2)}, u32[]{:S(2)}) collective-permute-start(bf16[480,512]{1,0:T(8,128)(2,1)S(1)} %constant_dynamic-update-slice_fusion), channel_id=1, source_target_pairs={{0,24},{1,7},{2,26},{3,1},{4,28},{5,3},{6,30},{7,5},{8,0},{9,15},{... | collective-permute-start | bytes 1474568 | tf_op jit(solution)/shard_map/ppermute | solution.py:30
  22.7 11.9 %collective-permute-start.11 = (bf16[320,512]{1,0:T(8,128)(2,1)S(1)}, bf16[320,512]{1,0:T(8,128)(2,1)S(1)}, u32[]{:S(2)}, u32[]{:S(2)}) collective-permute-start(bf16[320,512]{1,0:T(8,128)(2,1)S(1)} %constant_dynamic-update-slice_fusion.3.refs_0_), channel_id=1, source_target_pairs={{0,1},{1,0},{2,3},{3,2},{4,5},{5,4},{6,7},{7,6},{8,9},{9,8},{10,11... | collective-permute-start | bytes 983048 | tf_op jit(solution)/shard_map/ppermute | solution.py:35
  25.2 14.5 %collective-permute-start.8 = (bf16[640,512]{1,0:T(8,128)(2,1)S(1)}, bf16[640,512]{1,0:T(8,128)(2,1)S(1)}, u32[]{:S(2)}, u32[]{:S(2)}) collective-permute-start(bf16[640,512]{1,0:T(8,128)(2,1)S(1)} %collective-permute-done.7.refs_0_), channel_id=1, source_target_pairs={{0,1},{1,0},{2,3},{3,2},{4,5},{5,4},{6,7},{7,6},{8,9},{9,8},{10,11... | collective-permute-start | bytes 1966088 | tf_op jit(solution)/shard_map/ppermute | solution.py:35
  30.4 15.2 %collective-permute-start.4 = (bf16[480,512]{1,0:T(8,128)(2,1)S(1)}, bf16[480,512]{1,0:T(8,128)(2,1)S(1)}, u32[]{:S(2)}, u32[]{:S(2)}) collective-permute-start(bf16[480,512]{1,0:T(8,128)(2,1)S(1)} %collective-permute-done.3.refs_0_), channel_id=1, source_target_pairs={{0,1},{1,0},{2,3},{3,2},{4,5},{5,4},{6,7},{7,6},{8,9},{9,8},{10,11... | collective-permute-start | bytes 1474568 | tf_op jit(solution)/shard_map/ppermute | solution.py:35
  30.9 14.7 %collective-permute-start.6 = (bf16[480,512]{1,0:T(8,128)(2,1)S(1)}, bf16[480,512]{1,0:T(8,128)(2,1)S(1)}, u32[]{:S(2)}, u32[]{:S(2)}) collective-permute-start(bf16[480,512]{1,0:T(8,128)(2,1)S(1)} %collective-permute-done.5.refs_1_), channel_id=1, source_target_pairs={{0,1},{1,0},{2,3},{3,2},{4,5},{5,4},{6,7},{7,6},{8,9},{9,8},{10,11... | collective-permute-start | bytes 1474568 | tf_op jit(solution)/shard_map/ppermute | solution.py:35
  42.3 3.3 %copy-start.2 = (s32[512]{0:T(512)S(1)}, s32[512]{0:T(512)}, u32[]{:S(2)}) copy-start(s32[512]{0:T(512)} %param.10) | copy-start | bytes 6148
  45.7 18.7 %copy-start = (f32[512]{0:T(512)S(1)}, f32[512]{0:T(512)}, u32[]{:S(2)}) copy-start(f32[512]{0:T(512)} %param.11) | copy-start | bytes 6148
  45.8 18.6 %copy-start.1 = (f32[512]{0:T(512)S(1)}, f32[512]{0:T(512)}, u32[]{:S(2)}) copy-start(f32[512]{0:T(512)} %param.12) | copy-start | bytes 6148
  50.4 14.0 %all-to-all-start = ((f32[32,1,1536]{2,1,0:T(1,128)}), f32[32,1,1536]{2,1,0:T(1,128)S(1)}, u32[]{:S(2)}, u32[]{:S(2)}) async-start(f32[32,1,1536]{2,1,0:T(1,128)} %shard_map.117), calls=%async_computation | async-start | bytes 393216 | tf_op jit(solution)/shard_map/all_to_all | solution.py:363
  65.1 3.6 %collective-permute-start.13 = (f32[8,128]{1,0:T(8,128)S(1)}, f32[8,128]{1,0:T(8,128)S(1)}, u32[]{:S(2)}, u32[]{:S(2)}) collective-permute-start(f32[8,128]{1,0:T(8,128)S(1)} %get-tuple-element.31), channel_id=1, source_target_pairs={{0,32},{32,0},{64,96},{96,64},{1,33},{33,1},{65,97},{97,65},{2,34}... | collective-permute-start | bytes 12296 | tf_op jit(solution)/shard_map/ppermute | solution.py:377
  68.7 5.7 %collective-permute-start.14 = (f32[16,128]{1,0:T(8,128)S(1)}, f32[16,128]{1,0:T(8,128)S(1)}, u32[]{:S(2)}, u32[]{:S(2)}) collective-permute-start(f32[16,128]{1,0:T(8,128)S(1)} %pad_maximum_fusion.2), channel_id=1, source_target_pairs={{0,96},{32,64},{64,32},{96,0},{1,97},{33,65},{65,33},{97,1},{2,98}... | collective-permute-start | bytes 24584 | tf_op jit(solution)/shard_map/ppermute | solution.py:377
